TPU v7x, 32 devices: a whole 2x2x4 slice. The times are simulated.
32 devices in a mesh: group: 8 (over y, x, core), ep: 4 (over z).
Axes of the slice: x: 2, y: 2, z: 4, core: 2. Of those that a mesh axis runs over, the one named last changes fastest.
Arguments:
- tokens: bfloat16 [1024, 3584], P(('group', 'ep')), may hold values from -6 to 6
- expert_ids: int32 [1024, 8], P(('group', 'ep')), may hold values from 0 to 31, as said below
- gate_scores: float32 [1024, 8], P(('group', 'ep')), may hold values from 0.05 to 0.35
- replica_pick: int32 [1024, 8], P(('group', 'ep')), may hold values from 0 to 8
- replica_hot: int32 [4], replicated, may hold values from 0 to 7
- gate_weight: bfloat16 [32, 3584, 1024], P(('group', 'ep')), may hold values from -0.09375 to 0.09375
- up_weight: bfloat16 [32, 3584, 1024], P(('group', 'ep')), may hold values from -0.09375 to 0.09375
- down_weight: bfloat16 [32, 1024, 3584], P(('group', 'ep')), may hold values from -0.1875 to 0.1875
Outputs:
- mixed: bfloat16 [1024, 3584], P(('group', 'ep'))
- slot_load: float32 [32, 2], P(('group', 'ep'))
Inputs may be any that keep to these rules, and one draw needn't show every extreme that they name: `expert_ids`: each row names 8 different experts; in each aligned block of 16 rows (one micro-batch of one device) no expert is named by more than 5 rows, and the expert replica_hot[c] * 4 + c of each ep index c is named by exactly 5 rows.
All inputs are finite; a program needn't handle non-finite values.
Results may differ from a plain program's by a relative error of at most 0.0057.
Values may be sent and summed in bfloat16 or wider, within the bound.
A program may use at most 128 MiB of HBM per device.

v0:
```python
import functools

import jax
import jax.numpy as jnp
from jax import lax
from jax.experimental import pallas as pl
from jax.experimental.pallas import tpu as pltpu
from jax.sharding import PartitionSpec as P

AXES = ("group", "ep")
MESH = pl.DeviceIdType.MESH


def place_of(nplane, nep):
    group = lax.axis_index("group")
    ep = lax.axis_index("ep")
    core = lax.rem(group, 2)
    plane = lax.div(group, 2)

    def plane_peer(step):
        other = lax.rem(plane + step, nplane)
        return other, (other * 2 + core, ep)

    def ep_peer(step):
        other = lax.rem(ep + step, nep)
        return other, (group, other)

    return plane, ep, plane_peer, ep_peer


def greet(nplane, nep, plane_peer, ep_peer):
    barrier = pltpu.get_barrier_semaphore()
    for step in range(1, nplane):
        pl.semaphore_signal(barrier, inc=1, device_id=plane_peer(step)[1], device_id_type=MESH)
    for step in range(1, nep):
        pl.semaphore_signal(barrier, inc=1, device_id=ep_peer(step)[1], device_id_type=MESH)
    pl.semaphore_wait(barrier, nplane + nep - 2)


def gather_kernel(
    nplane, nep, cut, x_ref, note_ref, out_ref, notes_ref,
    own_sem, send_a, recv_a, send_b, recv_b, right_a, left_a, right_b, left_b, note_send, note_recv,
):
    plane, ep, plane_peer, ep_peer = place_of(nplane, nep)
    group = lax.axis_index("group")
    me = group * nep + ep
    total = 2 * nplane * nep
    width = x_ref.shape[1]
    cols = {"a": pl.ds(0, cut), "b": pl.ds(cut, width - cut)}
    recv = {"a": recv_a, "b": recv_b}
    rights = {"a": right_a, "b": right_b}
    lefts = {"a": left_a, "b": left_b}
    own = pltpu.make_async_copy(x_ref, out_ref.at[plane, ep], own_sem.at[0])
    own.start()
    own_note = pltpu.make_async_copy(note_ref, notes_ref.at[me], own_sem.at[1])
    own_note.start()

    barrier = pltpu.get_barrier_semaphore()
    for step in range(1, total):
        other = lax.rem(me + step, total)
        pl.semaphore_signal(
            barrier, inc=1, device_id=(lax.div(other, nep), lax.rem(other, nep)), device_id_type=MESH
        )
    pl.semaphore_wait(barrier, total - 1)

    def copy(src, p, e, half, send, target):
        return pltpu.make_async_remote_copy(
            src_ref=src.at[:, cols[half]],
            dst_ref=out_ref.at[p, e, :, cols[half]],
            send_sem=send,
            recv_sem=recv[half].at[p * nep + e],
            device_id=target,
            device_id_type=MESH,
        )

    sends = []
    used = {"a": 0, "b": 0}

    def push(src, p, e, half):
        send = send_a if half == "a" else send_b
        for step in range(1, nplane):
            made = copy(src, p, e, half, send.at[used[half]], plane_peer(step)[1])
            used[half] += 1
            made.start()
            sends.append(made)

    def arrived(p, e, half):
        copy(out_ref.at[p, e], p, e, half, send_a.at[0], ep_peer(1)[1]).wait_recv()

    def to_right(src, p, e, half):
        return copy(src, p, e, half, rights[half].at[p * nep + e], (group, lax.rem(ep + 1, nep)))

    def to_left(src, p, e, half):
        return copy(src, p, e, half, lefts[half].at[p * nep + e], (group, lax.rem(ep + nep - 1, nep)))

    has_right, has_left = ep < nep - 1, ep > 0

    def both_ways(src, p, half):
        @pl.when(has_right)
        def _():
            to_right(src, p, ep, half).start()

        @pl.when(has_left)
        def _():
            to_left(src, p, ep, half).start()

    def chain(p, back, half):
        @pl.when(ep - back >= 0)
        def _():
            arrived(p, ep - back, half)

            @pl.when(has_right)
            def _():
                to_right(out_ref.at[p, ep - back], p, ep - back, half).start()

        @pl.when(ep + back < nep)
        def _():
            arrived(p, ep + back, half)

            @pl.when(has_left)
            def _():
                to_left(out_ref.at[p, ep + back], p, ep + back, half).start()

    def chain_end(p, back, half):
        @pl.when((ep - back >= 0) & has_right)
        def _():
            to_right(out_ref.at[p, ep - back], p, ep - back, half).wait_send()

        @pl.when((ep + back < nep) & has_left)
        def _():
            to_left(out_ref.at[p, ep + back], p, ep + back, half).wait_send()

    def note(source, step, target):
        return pltpu.make_async_remote_copy(
            src_ref=note_ref,
            dst_ref=notes_ref.at[source],
            send_sem=note_send.at[step],
            recv_sem=note_recv.at[source],
            device_id=(lax.div(target, nep), lax.rem(target, nep)),
            device_id_type=MESH,
        )

    both_ways(x_ref, plane, "a")
    push(x_ref, plane, ep, "b")
    push(x_ref, plane, ep, "a")
    both_ways(x_ref, plane, "b")
    for step in range(1, total):
        note(me, step, lax.rem(me + step, total)).start()
    for back in range(1, max(nplane, nep)):
        if back < nep:
            chain(plane, back, "a")
        if back < nplane:
            source = lax.rem(plane + nplane - back, nplane)
            arrived(source, ep, "b")
            both_ways(out_ref.at[source, ep], source, "b")
        if back < nep:
            left_in, right_in = ep - back >= 0, ep + back < nep

            @pl.when(left_in)
            def _():
                for step in range(1, nplane):
                    copy(
                        out_ref.at[plane, ep - back], plane, ep - back, "a",
                        send_a.at[(nplane - 1) * back + step - 1], plane_peer(step)[1],
                    ).start()

            @pl.when(right_in)
            def _():
                for step in range(1, nplane):
                    copy(
                        out_ref.at[plane, ep + back], plane, ep + back, "a",
                        send_a.at[(nplane - 1) * (nep + back) + step - 1], plane_peer(step)[1],
                    ).start()
    for back in range(1, nep):
        for p_back in range(nplane):
            chain(lax.rem(plane + nplane - p_back, nplane), back, "b")
    for p_back in range(1, nplane):
        p = lax.rem(plane + nplane - p_back, nplane)
        for e in range(nep):
            arrived(p, e, "a")
    for step in range(1, total):
        source = lax.rem(me + total - step, total)
        note(source, step, lax.rem(me + 1, total)).wait_recv()
    for made in sends:
        made.wait_send()
    for back in range(1, nep):
        @pl.when(ep - back >= 0)
        def _():
            for step in range(1, nplane):
                copy(
                    out_ref.at[plane, ep - back], plane, ep - back, "a",
                    send_a.at[(nplane - 1) * back + step - 1], plane_peer(step)[1],
                ).wait_send()

        @pl.when(ep + back < nep)
        def _():
            for step in range(1, nplane):
                copy(
                    out_ref.at[plane, ep + back], plane, ep + back, "a",
                    send_a.at[(nplane - 1) * (nep + back) + step - 1], plane_peer(step)[1],
                ).wait_send()

    for back in range(nep):
        for half in ("a", "b"):
            for p_back in range(nplane if half == "b" else 1):
                p = lax.rem(plane + nplane - p_back, nplane)
                if back == 0:
                    @pl.when(has_right)
                    def _():
                        to_right(x_ref, p, ep, half).wait_send()

                    @pl.when(has_left)
                    def _():
                        to_left(x_ref, p, ep, half).wait_send()
                else:
                    chain_end(p, back, half)
    for step in range(1, total):
        note(me, step, lax.rem(me + step, total)).wait_send()
    own.wait()
    own_note.wait()


def gather_plane(tokens, note, nplane, nep, cut):
    rows, width = tokens.shape
    count = nplane * nep
    dma = pltpu.SemaphoreType.DMA
    vmem = pl.BlockSpec(memory_space=pltpu.VMEM)
    return pl.pallas_call(
        functools.partial(gather_kernel, nplane, nep, cut),
        out_shape=[
            jax.ShapeDtypeStruct((nplane, nep, rows, width), tokens.dtype),
            jax.ShapeDtypeStruct((2 * count,) + note.shape, note.dtype),
        ],
        in_specs=[vmem, vmem],
        out_specs=[vmem, vmem],
        scratch_shapes=[
            dma((2,)),
            dma((2 * (nplane - 1) * nep,)), dma((count,)), dma((nplane - 1,)), dma((count,)),
            dma((count,)), dma((count,)), dma((count,)), dma((count,)),
            dma((2 * count,)), dma((2 * count,)),
        ],
        compiler_params=pltpu.CompilerParams(collective_id=0, has_side_effects=True),
    )(tokens, note)


def scatter_kernel(
    nplane, nep, cut, part_ref, out_ref,
    land_a1, land_b1, mid_a, mid_b, land_a2, land_b2,
    send_a1, recv_a1, send_b1, recv_b1, send_a2, recv_a2, send_b2, recv_b2,
):
    plane, ep, plane_peer, ep_peer = place_of(nplane, nep)
    width = out_ref.shape[1]
    cols_a, cols_b = pl.ds(0, cut), pl.ds(cut, width - cut)
    greet(nplane, nep, plane_peer, ep_peer)

    def move(src, dst, send, recv, target):
        made = pltpu.make_async_remote_copy(
            src_ref=src, dst_ref=dst, send_sem=send, recv_sem=recv, device_id=target, device_id_type=MESH
        )
        made.start()
        return made

    first_a, first_b = {}, {}
    for item in range(1, max(nplane, nep) + 1):
        if item <= nep:
            e = lax.rem(ep + item, nep)
            for step in range(1, nplane):
                p, target = plane_peer(step)
                spot = (step - 1) * nep + item - 1
                first_a[item, step] = move(
                    part_ref.at[p, e, :, cols_a], land_a1.at[step - 1, item - 1],
                    send_a1.at[spot], recv_a1.at[spot], target,
                )
        if item <= nplane:
            p = lax.rem(plane + item, nplane)
            for step in range(1, nep):
                e, target = ep_peer(step)
                spot = (step - 1) * nplane + item - 1
                first_b[item, step] = move(
                    part_ref.at[p, e, :, cols_b], land_b1.at[step - 1, item - 1],
                    send_b1.at[spot], recv_b1.at[spot], target,
                )
    second_a, second_b = [], []
    for item in range(1, max(nplane, nep) + 1):
        if item <= nep:
            e, target = ep_peer(item)
            total = part_ref[plane, e, :, cols_a].astype(jnp.float32)
            for step in range(1, nplane):
                first_a[item, step].wait_recv()
                total = total + land_a1[step - 1, item - 1].astype(jnp.float32)
            if item < nep:
                mid_a[item - 1] = total.astype(mid_a.dtype)
                second_a.append(
                    move(mid_a.at[item - 1], land_a2.at[item - 1], send_a2.at[item - 1], recv_a2.at[item - 1], target)
                )
            else:
                total_a = total
        if item <= nplane:
            p, target = plane_peer(item)
            total = part_ref[p, ep, :, cols_b].astype(jnp.float32)
            for step in range(1, nep):
                first_b[item, step].wait_recv()
                total = total + land_b1[step - 1, item - 1].astype(jnp.float32)
            if item < nplane:
                mid_b[item - 1] = total.astype(mid_b.dtype)
                second_b.append(
                    move(mid_b.at[item - 1], land_b2.at[item - 1], send_b2.at[item - 1], recv_b2.at[item - 1], target)
                )
            else:
                total_b = total
    for index, made in enumerate(second_a):
        made.wait_recv()
        total_a = total_a + land_a2[index].astype(jnp.float32)
    out_ref[:, cols_a] = total_a.astype(out_ref.dtype)
    for index, made in enumerate(second_b):
        made.wait_recv()
        total_b = total_b + land_b2[index].astype(jnp.float32)
    out_ref[:, cols_b] = total_b.astype(out_ref.dtype)
    for made in list(first_a.values()) + list(first_b.values()) + second_a + second_b:
        made.wait_send()


def scatter_plane(parts, cut):
    nplane, nep, rows, width = parts.shape
    rest = width - cut
    kind = parts.dtype
    dma = pltpu.SemaphoreType.DMA
    pairs_a, pairs_b = (nplane - 1) * nep, (nep - 1) * nplane
    return pl.pallas_call(
        functools.partial(scatter_kernel, nplane, nep, cut),
        out_shape=jax.ShapeDtypeStruct((rows, width), kind),
        in_specs=[pl.BlockSpec(memory_space=pltpu.VMEM)],
        out_specs=pl.BlockSpec(memory_space=pltpu.VMEM),
        scratch_shapes=[
            pltpu.VMEM((nplane - 1, nep, rows, cut), kind),
            pltpu.VMEM((nep - 1, nplane, rows, rest), kind),
            pltpu.VMEM((nep - 1, rows, cut), kind),
            pltpu.VMEM((nplane - 1, rows, rest), kind),
            pltpu.VMEM((nep - 1, rows, cut), kind),
            pltpu.VMEM((nplane - 1, rows, rest), kind),
            dma((pairs_a,)), dma((pairs_a,)), dma((pairs_b,)), dma((pairs_b,)),
            dma((nep - 1,)), dma((nep - 1,)), dma((nplane - 1,)), dma((nplane - 1,)),
        ],
        compiler_params=pltpu.CompilerParams(collective_id=1, has_side_effects=True),
    )(parts)


def body(
    tokens, expert_ids, gate_scores, replica_pick, replica_hot, gate_weight, up_weight, down_weight
):
    ngroup = lax.axis_size("group")
    nep = lax.axis_size("ep")
    nplane = ngroup // 2
    device_count = ngroup * nep
    group_index = lax.axis_index("group")
    ep_index = lax.axis_index("ep")
    core = group_index % 2
    me = group_index * nep + ep_index
    partner = (group_index + 1 - 2 * core) * nep + ep_index
    tok_dev, width = tokens.shape
    top_count = expert_ids.shape[1]
    most = (tok_dev // 2 * top_count + device_count - 1) // device_count + 1
    capacity = 2 * most * nplane * nep
    cut = width // 256 * 128
    back_cut = width * 11 // 14 // 128 * 128

    coded = expert_ids * (ngroup + 1) + replica_pick
    note = jnp.concatenate([coded.astype(jnp.float32), gate_scores], axis=1).reshape(-1, 128)
    every, notes = gather_plane(tokens, note, nplane, nep, cut)
    every = every.reshape(nplane * nep * tok_dev, width)
    routing = notes.reshape(device_count * tok_dev, 2 * top_count)
    coded = routing[:, :top_count].astype(jnp.int32)
    ids = coded // (ngroup + 1)
    picks = coded % (ngroup + 1)
    hot = replica_hot[ep_index]
    replicated = (ids % nep == ep_index) & (ids // nep == hot) & (picks < ngroup)
    primary_load = jnp.sum(((ids == me) & ~replicated).astype(jnp.float32))
    replica_load = jnp.sum((replicated & (picks == group_index)).astype(jnp.float32))
    loads = jnp.stack([primary_load, replica_load])[None, :] / top_count

    mine = routing.reshape(nplane, 2, nep * tok_dev, 2 * top_count)
    mine = lax.dynamic_index_in_dim(mine, core, 1, keepdims=False).reshape(-1, 2 * top_count)
    my_ids = mine[:, :top_count].astype(jnp.int32) // (ngroup + 1)
    my_gates = mine[:, top_count:]

    def spots(expert):
        chosen = my_ids == expert
        mask = jnp.any(chosen, axis=1)
        scale = jnp.sum(jnp.where(chosen, my_gates, 0.0), axis=1)
        place = jnp.where(mask, jnp.cumsum(mask.astype(jnp.int32)) - 1, -1)
        spot = place[None, :] == jnp.arange(capacity, dtype=jnp.int32)[:, None]
        return spot, jnp.sum(jnp.where(spot, scale[None, :], 0.0), axis=1)

    spot_me, scale_me = spots(me)
    spot_other, scale_other = spots(partner)
    select = jnp.concatenate([spot_me, spot_other], axis=0).astype(jnp.bfloat16)
    row_scale = jnp.concatenate([scale_me, scale_other], axis=0)
    swap = [(index, index ^ 1) for index in range(ngroup)]

    picked = jnp.dot(select, every, preferred_element_type=jnp.float32).astype(jnp.bfloat16)
    inputs = jnp.concatenate(
        [picked[:capacity], lax.ppermute(picked[capacity:], "group", swap)], axis=0
    )
    gate_act = jnp.dot(inputs, gate_weight[0], preferred_element_type=jnp.float32)
    up_act = jnp.dot(inputs, up_weight[0], preferred_element_type=jnp.float32)
    hidden = (jax.nn.silu(gate_act) * up_act).astype(jnp.bfloat16)
    pair_out = jnp.dot(hidden, down_weight[0], preferred_element_type=jnp.float32).astype(jnp.bfloat16)
    pairs = jnp.concatenate(
        [pair_out[:capacity], lax.ppermute(pair_out[capacity:], "group", swap)], axis=0
    )
    scaled = (pairs.astype(jnp.float32) * row_scale[:, None]).astype(jnp.bfloat16)
    spread = lax.dot_general(
        select, scaled, (((0,), (0,)), ((), ())), preferred_element_type=jnp.float32
    ).astype(jnp.bfloat16)
    mixed = scatter_plane(spread.reshape(nplane, nep, tok_dev, width), back_cut)
    return mixed, loads


def solution(mesh):
    rows = P(AXES, None)
    weights = P(AXES, None, None)
    return jax.shard_map(
        body,
        mesh=mesh,
        in_specs=(rows, rows, rows, rows, P(), weights, weights, weights),
        out_specs=(rows, rows),
        check_vma=False,
    )
```

profile of v0, /device:TPU:0, one launch (start us, length us, event | category | flops | bytes accessed | tf_op | source)
XLA Modules:
  0.0 134.9 jit_solution(10892871573309167763)
XLA Ops:
  0.7 0.7 add_convert_fusion
  1.4 0.7 pad_maximum_fusion.7
  2.1 0.1 copy.13
  2.1 0.7 reshape.115.note_ref
  2.8 51.5 %shard_map.95 = (bf16[4,4,32,3584]{3,2,1,0:T(8,128)(2,1)}, f32[32,4,128]{2,1,0:T(4,128)}) custom-call(bf16[32,3584]{1,0:T(8,128)(2,1)} %x_ref.1, f32[4,128]{1,0:T(4,128)} %reshape.115.note_ref), custom_call_target="tpu_custom_call" | custom-call | tf_op jit(solution)/shard_map/pallas_call | solution.py:228
  54.3 1.0 reshape_reshape.3
  55.4 0.1 fusion.35
  55.5 0.1 copy.17
  55.6 0.1 copy.18
  55.8 0.3 reduce-window.24
  56.1 0.1 slice.38
  56.2 0.1 slice_reduce_fusion
  56.3 0.1 bitcast_select_fusion
  56.4 0.3 reduce-window.16
  56.7 0.1 slice.36
  56.8 0.1 slice_reduce_fusion.1
  57.0 0.1 bitcast_select_fusion.1
  57.0 0.1 iota_compare_fusion
  57.1 0.0 copy-start.1
  57.2 0.0 copy-start.2
  57.2 0.6 copy-done.1
  57.8 0.0 copy-done.2
  57.8 3.4 %convolution_convert_fusion.1 = bf16[320,3584]{1,0:T(8,128)(2,1)S(1)} fusion(bf16[512,3584]{1,0:T(8,128)(2,1)} %bitcast.34, pred[160,512]{1,0:T(32,128)(4,1)S(1)} %get-tuple-element.20, pred[160,512]{1,0:T(32,128)(4,1)S(1)} %get-tuple-element.21), kind=kOutput, calls=%fused_computation.8 | convolution fusion | flops 1175715840 | bytes 6127616 | tf_op jit(solution)/shard_map/dot_general | solution.py:400
  61.2 0.1 fusion.34
  61.4 0.1 collective-permute-start
  61.4 2.8 %collective-permute-done = bf16[160,3584]{1,0:T(8,128)(2,1)S(1)} collective-permute-done((bf16[160,3584]{1,0:T(8,128)(2,1)S(1)}, bf16[160,3584]{1,0:T(8,128)(2,1)S(1)}, u32[]{:S(2)}, u32[]{:S(2)}) %collective-permute-start) | collective-permute-done | bytes 1146912 | tf_op jit(solution)/shard_map/ppermute | solution.py:402
  64.2 0.0 copy-start.3
  64.2 1.0 copy-done.3
  65.2 6.7 %fusion.2 = f32[320,1024]{1,0:T(8,128)} fusion(bf16[1,3584,1024]{2,1,0:T(8,128)(2,1)} %param.14, bf16[160,3584]{1,0:T(8,128)(2,1)S(1)} %collective-permute-done, bf16[160,3584]{1,0:T(8,128)(2,1)S(1)} %get-tuple-element.14), kind=kOutput, calls=%fused_computation.2 | convolution fusion | flops 2353397760 | bytes 10944512 | tf_op jit(solution)/shard_map/dot_general | solution.py:405
  71.9 10.8 %fusion.6 = bf16[320,3584]{1,0:T(8,128)(2,1)S(1)} fusion(bf16[1,1024,3584]{2,1,0:T(8,128)(2,1)} %param.15, f32[320,1024]{1,0:T(8,128)} %fusion.2, bf16[1,3584,1024]{2,1,0:T(8,128)(2,1)} %param.13, bf16[160,3584]{1,0:T(8,128)(2,1)} %copy-done.3, bf16[160,3584]{1,0:T(8,128)(2,1)S(1)} %get-tuple-element.14), kind=kOutput, calls=%fused_computation.7 | convolution fusion | flops 4705320960 | bytes 20578304 | tf_op jit(solution)/shard_map/dot_general | solution.py:407
  82.7 0.0 copy-start
  82.7 0.0 copy-start.4
  82.7 1.2 fusion.33
  83.9 0.1 collective-permute-start.1
  84.0 0.0 copy-done
  84.0 0.2 reshape.121
  84.2 0.2 copy.19
  84.4 0.0 copy-done.4
  84.4 0.6 dynamic_slice.8
  85.0 1.4 %convert_reduce_fusion.1 = (f32[]{:T(128)}, f32[]{:T(128)}) fusion(s32[]{:T(128)S(6)} %add.55, f32[1024,8]{0,1:T(8,128)S(1)} %copy.19, s32[]{:T(128)S(6)} %axis_index.23, s32[]{:T(128)} %bitcast.10, s32[]{:T(128)S(6)} %axis_index.25), kind=kLoop, calls=%fused_computation.32 | loop fusion | flops 376830 | bytes 32792 | tf_op jit(solution)/shard_map/reduce_sum | solution.py:377
  86.4 1.8 %maximum_multiply_fusion = f32[1,2]{1,0:T(1,128)} fusion(f32[1,1]{1,0:T(1,128)} %bitcast.12, f32[1,1]{1,0:T(1,128)} %bitcast.11), kind=kLoop, calls=%fused_computation.58 | loop fusion | flops 4 | bytes 16 | tf_op jit(solution)/shard_map/div | solution.py:379
  88.2 0.2 select_reduce_fusion
  88.4 0.1 pad_maximum_fusion.8
  88.4 0.0 collective-permute-done.1
  88.4 4.9 %convolution_convert_fusion = bf16[512,3584]{1,0:T(8,128)(2,1)} fusion(bf16[160,3584]{1,0:T(8,128)(2,1)S(1)} %collective-permute-done.1, bf16[160,3584]{1,0:T(8,128)(2,1)S(1)} %get-tuple-element.12, f32[320]{0:T(512)S(1)} %pad_maximum_fusion.8, pred[160,512]{1,0:T(32,128)(4,1)} %copy-done.1, pred[160,512]{1,0:T(32,128)(4,1)} %copy-done.2), kind=kOutput, calls=%fused_computation.6 | convolution fusion | flops 1183285248 | bytes 6128896 | tf_op jit(solution)/shard_map/dot_general | solution.py:412
  93.4 39.9 %shard_map.96 = bf16[32,3584]{1,0:T(8,128)(2,1)} custom-call(bf16[4,4,32,3584]{3,2,1,0:T(8,128)(2,1)} %bitcast.31), custom_call_target="tpu_custom_call" | custom-call | tf_op jit(solution)/shard_map/pallas_call | solution.py:329
  133.2 1.6 %copy.27 = bf16[32,3584]{1,0:T(8,128)(2,1)} copy(bf16[32,3584]{1,0:T(8,128)(2,1)} %shard_map.96) | data formatting | bytes 458752
  (8 shorter events, 0.2 us)
Async XLA Ops:
  57.1 0.6 copy-start.1
  57.2 0.6 copy-start.2
  61.4 2.9 %collective-permute-start = (bf16[160,3584]{1,0:T(8,128)(2,1)S(1)}, bf16[160,3584]{1,0:T(8,128)(2,1)S(1)}, u32[]{:S(2)}, u32[]{:S(2)}) collective-permute-start(bf16[160,3584]{1,0:T(8,128)(2,1)S(1)} %get-tuple-element.15), channel_id=1, source_target_pairs={{0,4},{4,0},{8,12},{12,8},{16,20},{20,16},{24,28},{28,24},{1,5},{5... | collective-permute-start | bytes 3440648 | tf_op jit(solution)/shard_map/ppermute | solution.py:402
  64.2 1.0 copy-start.3
  82.7 1.3 copy-start
  82.7 1.7 %copy-start.4 = (s32[4]{0:T(128)S(1)}, s32[4]{0:T(128)}, u32[]{:S(2)}) copy-start(s32[4]{0:T(128)} %param.12) | copy-start | bytes 52
  83.9 4.6 %collective-permute-start.1 = (bf16[160,3584]{1,0:T(8,128)(2,1)}, bf16[160,3584]{1,0:T(8,128)(2,1)S(1)}, u32[]{:S(2)}, u32[]{:S(2)}) collective-permute-start(bf16[160,3584]{1,0:T(8,128)(2,1)} %get-tuple-element.13), channel_id=1, source_target_pairs={{0,4},{4,0},{8,12},{12,8},{16,20},{20,16},{24,28},{28,24},{1,5},{5... | collective-permute-start | bytes 3440648 | tf_op jit(solution)/shard_map/ppermute | solution.py:409
where the time goes:
time: 135 us
  Pallas kernels  91.3 us (68%)
  matrix products  25.8 us (19%)
  local copies, waits for them, and re-layouts  8.08 us (6%)
  other arithmetic  5.89 us (4%)
  waiting for transfers between devices  2.79 us (2%)
    pallas_call x1, Pallas kernels, gather_plane(): pl.pallas_call(functools.partial(gather_kernel, nplane, nep, cut), out_sh...  51.5 us
    pallas_call x1, Pallas kernels, scatter_plane(): pl.pallas_call(functools.partial(scatter_kernel, nplane, nep, cut), out_s...  39.9 us
    dot_general x1, matrix products, body(): jnp.dot(hidden, down_weight[0], preferred_element_type=jnp.float32)  10.8 us
    dot_general x1, matrix products, body(): up_act = jnp.dot(inputs, up_weight[0], preferred_element_type=jnp.float32)  6.67 us
    dot_general x1, matrix products, body(): lax.dot_general(select, scaled, (((0,), (0,)), ((), ())), preferred_eleme...  4.92 us
    unnamed x14, local copies, waits for them, and re-layouts  3.67 us
    dot_general x1, matrix products, body(): jnp.dot(select, every, preferred_element_type=jnp.float32)  3.38 us
    ppermute x1, waiting for transfers between devices, body(): lax.ppermute(picked[capacity:], 'group', swap)  2.79 us
  transfers between devices with their start and end apart: 2, of which 1 were waited for; matrix products, arithmetic and copies ran while one was open for 3% of the time, Pallas kernels for 0%

commit v1 on v0

--- a/solution.py
+++ b/solution.py
@@ -1,4 +1,5 @@
 import functools
+import math
 
 import jax
 import jax.numpy as jnp
@@ -9,6 +10,13 @@
 
 AXES = ("group", "ep")
 MESH = pl.DeviceIdType.MESH
+
+LINE_STEP, RING_STEP, DEEP_STEP, PRODUCT_STEP = 1.1, 3.1, 2.3, 2.6
+SPREAD_STEP, BACK_RING, BACK_LINE, BACK_DEEP = 2.0, 2.0, 2.0, 2.0
+PIECES = 2
+INTO = (("line", 4, 5.0), ("line", 4, 0.0), ("line", 3, 0.0), ("ring", 3, 0.0))
+OUTOF = (("ring", 3, 0.0), ("line", 4, 1.0), ("line", 4, 4.0), ("line", 3, 8.0))
+VMEM_LIMIT = 67043328
 
 
 def place_of(nplane, nep):
@@ -345,6 +353,654 @@
     )(parts)
 
 
+def ring_spot(nplane, index):
+    half = nplane // 2
+    return lax.select(index < half, 2 * index, 2 * (nplane - 1 - index) + 1)
+
+
+def ring_index(nplane, plane):
+    row = lax.div(plane, 2)
+    return lax.select(lax.rem(plane, 2) == 0, row, nplane - 1 - row)
+
+
+def offsets(nep):
+    return [0] + [side * back for back in range(1, nep) for side in (-1, 1)]
+
+
+def gather_order(parts, nplane, nep):
+    far = nplane // 2
+    events = []
+    for off in offsets(nep):
+        at = LINE_STEP * abs(off)
+        if off:
+            events.append((at, 1, ("note line", 0, 0, off, 0)))
+        for d in range(1, far + 1):
+            events.append((at + RING_STEP * d, 1 + d, ("note ring", 0, 0, off, d)))
+    events.append((LINE_STEP * (nep - 1) + RING_STEP * far, 2 + far, ("tables", 0, 0, 0, 0)))
+    for index, (kind, _, _, start) in enumerate(parts):
+        events.append((start, 0, ("own", index, 0, 0, 0)))
+        last = start
+        if kind == "line":
+            for off in offsets(nep):
+                at = start + LINE_STEP * abs(off)
+                if off:
+                    events.append((at, 1, ("line", index, 0, off, 0)))
+                for d in range(1, far + 1):
+                    last = max(last, at + RING_STEP * d)
+                    events.append((at + RING_STEP * d, 1 + d, ("ring", index, 0, off, d)))
+        else:
+            for d in range(1, far + 1):
+                events.append((start + RING_STEP * d, 1 + d, ("ring", index, 0, 0, d)))
+            for q in range(nplane):
+                for off in offsets(nep)[1:]:
+                    at = start + RING_STEP * min(q, nplane - q) + DEEP_STEP * abs(off)
+                    last = max(last, at)
+                    events.append((at, 2 + far, ("line", index, q, off, 0)))
+        events.append((last, 3 + far, ("pick", index, 0, 0, 0)))
+        for piece in range(PIECES):
+            events.append((last + PRODUCT_STEP * (piece + 1), 4 + far, ("product", index, piece, 0, 0)))
+    events.sort()
+    return [event for _, _, event in events]
+
+
+def scatter_order(parts, nplane, nep):
+    far = nplane // 2
+    events = []
+    for index, (kind, _, _, start) in enumerate(parts):
+        events.append((start, 0, ("down", index, 0, 0, 0)))
+        begin = start + SPREAD_STEP
+        events.append((begin, 1, ("spread", index, 0, 0, 0)))
+        if kind == "line":
+            for off in offsets(nep):
+                for d in range(far, -1, -1):
+                    at = begin + BACK_RING * (far - d)
+                    if d == 0:
+                        at = at + BACK_LINE * (nep - 1 - abs(off))
+                    events.append((at, 2 + nep - abs(off), ("ring", index, 0, off, d)))
+        else:
+            for q in range(nplane):
+                for off in offsets(nep):
+                    at = begin + BACK_DEEP * (nep - 1 - abs(off))
+                    events.append((at, 2 + nep - abs(off), ("line", index, q, off, 0)))
+            done = begin + BACK_DEEP * (nep - 1)
+            for d in range(far, -1, -1):
+                events.append((done + BACK_RING * (far - d), 3 + nep, ("ring", index, 0, 0, d)))
+    events.sort(key=lambda event: (event[0], event[1], event[2][1], event[2][2], -event[2][3], -event[2][4]))
+    return [event for _, _, event in events]
+
+
+def layer_kernel(
+    plan, hot_ref, tok_ref, ids_ref, picks_ref, gates_ref, wg_hbm, wu_hbm, wd_hbm, out_ref, load_ref,
+    xs, notes, route, sel, back, wg, wu, wd, inputs, stage, acc_g, acc_u, hidden, pairs, stage2, parts_ref,
+    ring_land, line_land, count_own, count_in,
+    own_sem, w_sem, note_recv, note_send, x_recv, x_send, swap_send, swap_recv, ring_recv, line_recv, out_send,
+):
+    nplane, nep, most, into, outof = plan
+    far = nplane // 2
+    count = nplane * nep
+    rows, width = out_ref.shape
+    top = ids_ref.shape[0]
+    total = count * rows
+    cap = stage.shape[0]
+    ngroup = 2 * nplane
+    group = lax.axis_index("group")
+    ep = lax.axis_index("ep")
+    core = lax.rem(group, 2)
+    me_ring = ring_index(nplane, lax.div(group, 2))
+    partner_group = group + 1 - 2 * core
+    partner = (partner_group, ep)
+    f32 = jnp.float32
+    bf16 = jnp.bfloat16
+
+    def spot(q):
+        return lax.rem(me_ring + q + nplane, nplane)
+
+    def ring_peer(side):
+        return (ring_spot(nplane, spot(side)) * 2 + core, ep)
+
+    peers = {1: ring_peer(1), -1: ring_peer(-1)}
+    line_peers = {1: (group, lax.min(ep + 1, nep - 1)), -1: (group, lax.max(ep - 1, 0))}
+    has = {1: ep < nep - 1, -1: ep > 0}
+
+    def valid(off):
+        if off == 0:
+            return None
+        return (ep + off < nep) if off > 0 else (ep + off >= 0)
+
+    def both(a, b):
+        if a is None:
+            return b
+        return a if b is None else a & b
+
+    def when(cond, run):
+        if cond is None:
+            run()
+        else:
+            pl.when(cond)(run)
+
+    waits = []
+
+    def copy(src, dst, send, recv, target):
+        return pltpu.make_async_remote_copy(
+            src_ref=src, dst_ref=dst, send_sem=send, recv_sem=recv, device_id=target, device_id_type=MESH
+        )
+
+    def launch(cond, make):
+        when(cond, lambda: make().start())
+        waits.append((cond, make))
+
+    own_block = me_ring * nep + ep
+    own_copies = []
+    for index, (_, c0, cols, _) in enumerate(into):
+        made = pltpu.make_async_copy(
+            tok_ref.at[:, pl.ds(c0, cols)], xs.at[own_block, :, pl.ds(c0, cols)], own_sem.at[index]
+        )
+        made.start()
+        own_copies.append(made)
+    weight_copies = []
+    for index, (src, dst) in enumerate(((wg_hbm, wg), (wu_hbm, wu), (wd_hbm, wd))):
+        made = pltpu.make_async_copy(src, dst, w_sem.at[index])
+        made.start()
+        weight_copies.append(made)
+
+    barrier = pltpu.get_barrier_semaphore()
+    for target in (partner, peers[1], peers[-1]):
+        pl.semaphore_signal(barrier, inc=1, device_id=target, device_id_type=MESH)
+    for side in (1, -1):
+        @pl.when(has[side])
+        def _(side=side):
+            pl.semaphore_signal(barrier, inc=1, device_id=line_peers[side], device_id_type=MESH)
+
+    note = notes.at[own_block]
+    note[...] = jnp.zeros(note.shape, f32)
+    note[:, pl.ds(0, rows)] = ids_ref[...].astype(f32)
+    note[:, pl.ds(rows, rows)] = picks_ref[...].astype(f32)
+    note[:, pl.ds(2 * rows, rows)] = gates_ref[...]
+    pl.semaphore_wait(barrier, 3 + has[1].astype(jnp.int32) + has[-1].astype(jnp.int32))
+
+    used = {"note": 0, "x": 0, "out": 0}
+
+    def place(index, half, block):
+        return x_recv.at[index, half, block]
+
+    def x_copy(index, half, block, cols, send, target):
+        part = xs.at[block, :, pl.ds(cols[0], cols[1])]
+        return copy(part, part, x_send.at[send], place(index, half, block), target)
+
+    def x_launch(cond, index, half, block, cols, target):
+        send = used["x"]
+        used["x"] += 1
+        launch(cond, lambda: x_copy(index, half, block, cols, send, target))
+
+    def x_wait(index, half, block, cols):
+        x_copy(index, half, block, cols, 0, partner).wait_recv()
+
+    def halves(c0, cols):
+        return {1: (0, (c0, cols // 2)), -1: (1, (c0 + cols // 2, cols // 2))}
+
+    def ring_out(cond, index, block, side, d):
+        _, c0, cols, _ = into[index]
+        half, span = (0, (c0, cols)) if d < far else halves(c0, cols)[side]
+        x_launch(cond, index, half, block, span, peers[side])
+
+    def line_out(index, q, off, side):
+        _, c0, cols, _ = into[index]
+        cond = both(valid(off), has[side])
+        x_launch(cond, index, 0, spot(q) * nep + ep + off, (c0, cols), line_peers[side])
+
+    def note_launch(cond, block, target):
+        send = used["note"]
+        used["note"] += 1
+        launch(cond, lambda: copy(
+            notes.at[block], notes.at[block], note_send.at[send], note_recv.at[block], target))
+
+    def note_wait(block):
+        copy(notes.at[block], notes.at[block], note_send.at[0], note_recv.at[block], partner).wait_recv()
+
+    def note_own():
+        for side in (1, -1):
+            note_launch(has[side], own_block, line_peers[side])
+        for side in (1, -1):
+            if far > 1 or side > 0:
+                note_launch(None, own_block, peers[side])
+
+    def note_line(off):
+        block = me_ring * nep + ep + off
+        when(valid(off), lambda: note_wait(block))
+        side = 1 if off < 0 else -1
+        note_launch(both(valid(off), has[side]), block, line_peers[side])
+        for way in (1, -1):
+            if far > 1 or way > 0:
+                note_launch(valid(off), block, peers[way])
+
+    def note_ring(off, d):
+        for side in (1, -1):
+            if d == far and side < 0:
+                continue
+            block = spot(-side * d) * nep + ep + off
+            when(valid(off), lambda: note_wait(block))
+            if d < far and (d + 1 < far or side > 0):
+                note_launch(valid(off), block, peers[side])
+
+    def gather_own(index):
+        own_copies[index].wait()
+        for side in (1, -1):
+            line_out(index, 0, 0, side)
+        for side in (1, -1):
+            ring_out(None, index, own_block, side, 1)
+
+    def gather_line(index, q, off):
+        kind, c0, cols, _ = into[index]
+        block = spot(q) * nep + ep + off
+        when(valid(off), lambda: x_wait(index, 0, block, (c0, cols)))
+        line_out(index, q, off, 1 if off < 0 else -1)
+        if kind == "line":
+            for side in (1, -1):
+                ring_out(valid(off), index, block, side, 1)
+
+    def gather_ring(index, off, d):
+        kind, c0, cols, _ = into[index]
+        for side in (1, -1):
+            block = spot(-side * d) * nep + ep + off
+            half, span = (0, (c0, cols)) if d < far else halves(c0, cols)[side]
+            when(valid(off), lambda: x_wait(index, half, block, span))
+            if d < far:
+                ring_out(valid(off), index, block, side, d + 1)
+                if kind == "ring":
+                    for way in (1, -1):
+                        line_out(index, -side * d, 0, way)
+        if d == far and kind == "ring":
+            for way in (1, -1):
+                line_out(index, far, 0, way)
+
+    def tables():
+        lane = lax.broadcasted_iota(jnp.int32, (top, 128), 1)
+        fit = 128 // rows
+        for chunk in range(total // 128):
+            for what in range(3):
+                piece = jnp.zeros((top, 128), f32)
+                for j in range(fit):
+                    tile = notes[chunk * fit + j]
+                    turn = (rows * (j - what)) % 128
+                    if turn:
+                        tile = pltpu.roll(tile, turn, 1)
+                    piece = jnp.where(lax.div(lane, rows) == j, tile, piece)
+                route[what, :, pl.ds(chunk * 128, 128)] = piece
+        expert = group * nep + ep
+        other = partner_group * nep + ep
+        hot = (hot_ref[ep] * nep + ep).astype(f32)
+        expert_f, other_f = expert.astype(f32), other.astype(f32)
+        block_rows = rows // 2
+        a = lax.broadcasted_iota(jnp.int32, (128, 128), 0)
+        b = lax.broadcasted_iota(jnp.int32, (128, 128), 1)
+        before = ((lax.div(a, block_rows) == lax.div(b, block_rows)) & (a < b)).astype(f32)
+        sub = lax.broadcasted_iota(jnp.int32, (8, 128), 0)
+        lane8 = lax.broadcasted_iota(jnp.int32, (8, 128), 1)
+        slot = lax.broadcasted_iota(jnp.int32, (cap, 128), 0).astype(f32)
+        sums = [jnp.zeros((1, 1), f32) for _ in range(4)]
+
+        def add_up(flag):
+            return jnp.sum(jnp.sum(flag.astype(f32), axis=1, keepdims=True), axis=0, keepdims=True)
+
+        for chunk in range(total // 128):
+            at = pl.ds(chunk * 128, 128)
+            ids, picks, gates = route[0, :, at], route[1, :, at], route[2, :, at]
+            chosen = [ids == expert_f, ids == other_f]
+            flag = [jnp.sum(c.astype(f32), axis=0, keepdims=True) for c in chosen]
+            scale = [jnp.sum(jnp.where(c, gates, 0.0), axis=0, keepdims=True) for c in chosen]
+            stacked = jnp.where(sub == 0, flag[0], jnp.where(sub == 1, flag[1], 0.0))
+            rank = jnp.dot(stacked, before, preferred_element_type=f32)
+            first = (lax.div(lane8[0:1], block_rows) + chunk * (128 // block_rows)).astype(f32) * most
+            scaled = []
+            for which in range(2):
+                position = jnp.where(flag[which] > 0, first + rank[which:which + 1], -1.0)
+                one = (slot == position).astype(f32)
+                sel[pl.ds(which * cap, cap), at] = one.astype(bf16)
+                scaled.append(one * scale[which])
+            back[at, :] = jnp.concatenate(scaled, axis=0).T.astype(bf16)
+            copied = (ids == hot) & (picks < ngroup)
+            for which, (here, its) in enumerate(((expert_f, group), (other_f, partner_group))):
+                sums[2 * which] = sums[2 * which] + add_up((ids == here) & ~copied)
+                sums[2 * which + 1] = sums[2 * which + 1] + add_up(copied & (picks == its.astype(f32)))
+        lane_n = lane8
+        count_own[0] = jnp.where(lane_n == 0, sums[0], jnp.where(lane_n == 1, sums[1], 0.0))
+        count_own[1] = jnp.where(lane_n == 0, sums[2], jnp.where(lane_n == 1, sums[3], 0.0))
+        launch(None, count_copy)
+
+    def count_copy():
+        spare = len(into) + len(outof)
+        return copy(count_own.at[1], count_in, swap_send.at[spare], swap_recv.at[spare], partner)
+
+    step = 256
+
+    def in_copy(index):
+        _, c0, cols, _ = into[index]
+        return copy(
+            stage.at[:, pl.ds(c0, cols)], inputs.at[pl.ds(cap, cap), pl.ds(c0, cols)],
+            swap_send.at[index], swap_recv.at[index], partner,
+        )
+
+    def pick(index):
+        _, c0, cols, _ = into[index]
+
+        def part(i, _):
+            at = pl.ds(pl.multiple_of(c0 + i * step, step), step)
+            got = jnp.dot(sel[...], xs[:, :, at].reshape(total, step), preferred_element_type=f32).astype(bf16)
+            inputs[pl.ds(0, cap), at] = got[:cap]
+            stage[:, at] = got[cap:]
+            return 0
+
+        lax.fori_loop(0, cols // step, part, 0)
+        launch(None, lambda: in_copy(index))
+
+    seen = []
+
+    def product(index, piece):
+        _, c0, cols, _ = into[index]
+        if piece == 0:
+            in_copy(index).wait_recv()
+            if not seen:
+                weight_copies[0].wait()
+                weight_copies[1].wait()
+        first = piece not in seen
+        seen.append(piece)
+        tiles = acc_g.shape[1] // step // PIECES
+
+        def part(j, _):
+            at = pl.ds(pl.multiple_of((piece * tiles + j) * step, step), step)
+            for weight, acc in ((wg, acc_g), (wu, acc_u)):
+                got = jnp.dot(
+                    inputs[:, pl.ds(c0, cols)], weight[pl.ds(c0, cols), at], preferred_element_type=f32
+                )
+                acc[:, at] = got if first else acc[:, at] + got
+            return 0
+
+        lax.fori_loop(0, tiles, part, 0)
+
+    def activate():
+        def part(i, _):
+            at = pl.ds(pl.multiple_of(i * 32, 32), 32)
+            gate = acc_g[at, :]
+            hidden[at, :] = (gate / (1.0 + jnp.exp(-gate)) * acc_u[at, :]).astype(bf16)
+            return 0
+
+        lax.fori_loop(0, 2 * cap // 32, part, 0)
+
+    def back_copy(index):
+        _, c0, cols, _ = outof[index]
+        spot_of = len(into) + index
+        return copy(
+            stage2.at[:, pl.ds(c0, cols)], pairs.at[pl.ds(cap, cap), pl.ds(c0, cols)],
+            swap_send.at[spot_of], swap_recv.at[spot_of], partner,
+        )
+
+    def down(index):
+        _, c0, cols, _ = outof[index]
+
+        def part(i, _):
+            at = pl.ds(pl.multiple_of(c0 + i * step, step), step)
+            got = jnp.dot(hidden[...], wd[:, at], preferred_element_type=f32).astype(bf16)
+            pairs[pl.ds(0, cap), at] = got[:cap]
+            stage2[:, at] = got[cap:]
+            return 0
+
+        lax.fori_loop(0, cols // step, part, 0)
+        launch(None, lambda: back_copy(index))
+
+    def spread(index):
+        _, c0, cols, _ = outof[index]
+        back_copy(index).wait_recv()
+
+        def part(i, _):
+            at = pl.ds(pl.multiple_of(c0 + i * step, step), step)
+            got = jnp.dot(back[...], pairs[:, at], preferred_element_type=f32).astype(bf16)
+            parts_ref[:, :, at] = got.reshape(count, rows, step)
+            return 0
+
+        lax.fori_loop(0, cols // step, part, 0)
+
+    def add(dst, sources):
+        def part(i, _):
+            at = pl.ds(pl.multiple_of(i * 16, 16), 16)
+            value = sources[0][at, :].astype(f32)
+            for source in sources[1:]:
+                value = value + source[at, :].astype(f32)
+            dst[at, :] = value.astype(dst.dtype)
+            return 0
+
+        lax.fori_loop(0, rows // 16, part, 0)
+
+    def out_launch(cond, src, dst, recv, target):
+        send = used["out"]
+        used["out"] += 1
+        launch(cond, lambda: copy(src, dst, out_send.at[send], recv, target))
+
+    def way(side):
+        return 0 if side > 0 else 1
+
+    def ring_slot(index, side, d, half, e, span):
+        c0, cols = span
+        return (
+            ring_land.at[way(side), d, e, :, pl.ds(c0, cols)],
+            ring_recv.at[index, way(side), d, half, e],
+        )
+
+    def ring_send(cond, index, off, side, d, half, span):
+        dst, recv = ring_slot(index, side, d - 1, half, ep + off, span)
+        src = parts_ref.at[spot(side * d) * nep + ep + off, :, pl.ds(span[0], span[1])]
+        out_launch(cond, src, dst, recv, peers[side])
+
+    def ring_await(index, off, side, d, half, span):
+        dst, recv = ring_slot(index, side, d, half, ep + off, span)
+        copy(dst, dst, out_send.at[0], recv, partner).wait_recv()
+        return dst
+
+    def line_slot(index, side, q, e, span):
+        c0, cols = span
+        return (
+            line_land.at[way(side), spot(q) * nep + e, :, pl.ds(c0, cols)],
+            line_recv.at[index, way(side), spot(q) * nep + e],
+        )
+
+    def line_send(cond, index, q, off, side):
+        _, c0, cols, _ = outof[index]
+        dst, recv = line_slot(index, side, q, ep + off, (c0, cols))
+        src = parts_ref.at[spot(q) * nep + ep + off, :, pl.ds(c0, cols)]
+        out_launch(cond, src, dst, recv, line_peers[side])
+
+    def line_await(index, side, q, off):
+        _, c0, cols, _ = outof[index]
+        dst, recv = line_slot(index, side, q, ep + off, (c0, cols))
+        copy(dst, dst, out_send.at[0], recv, partner).wait_recv()
+        return dst
+
+    def block(q, off, span):
+        return parts_ref.at[spot(q) * nep + ep + off, :, pl.ds(span[0], span[1])]
+
+    def line_merge(index, q, off, sources, dst):
+        left, right = has[-1], has[1]
+        if off != 0:
+            side = 1 if off > 0 else -1
+            behind = has[-side]
+
+            def go():
+                @pl.when(behind)
+                def _():
+                    add(dst, sources + [line_await(index, side, q, off)])
+
+                if len(sources) > 1:
+                    @pl.when(jnp.logical_not(behind))
+                    def _():
+                        add(dst, sources)
+
+            when(valid(off), go)
+            line_send(valid(off), index, q, off, side)
+        else:
+            @pl.when(left & right)
+            def _():
+                add(dst, sources + [line_await(index, 1, q, 0), line_await(index, -1, q, 0)])
+
+            @pl.when(left & jnp.logical_not(right))
+            def _():
+                add(dst, sources + [line_await(index, 1, q, 0)])
+
+            @pl.when(right & jnp.logical_not(left))
+            def _():
+                add(dst, sources + [line_await(index, -1, q, 0)])
+
+    def scatter_ring(index, off, d):
+        kind, c0, cols, _ = outof[index]
+        whole = (c0, cols)
+        split = halves(c0, cols)
+        if d == far:
+            for side in (1, -1):
+                half, span = split[side]
+                ring_send(valid(off), index, off, side, d, half, span)
+            if far > 1:
+                for side in (1, -1):
+                    half, span = split[-side]
+                    ring_send(valid(off), index, off, side, d - 1, half, span)
+        elif d > 0:
+            for side in (1, -1):
+                pieces = [split[side]] if d + 1 == far else [split[1], split[-1]]
+                for half, span in pieces:
+                    def go(half=half, span=span, side=side):
+                        got = ring_await(index, off, side, d, half, span)
+                        add(block(side * d, off, span), [block(side * d, off, span), got])
+
+                    when(valid(off), go)
+                    ring_send(valid(off), index, off, side, d, half, span)
+        else:
+            def take():
+                pieces = {}
+                for side in (1, -1):
+                    for half, span in ([split[side]] if far == 1 else [split[1], split[-1]]):
+                        ring_await(index, off, side, 0, half, span)
+
+            when(valid(off), take)
+            sources = [block(0, off, whole)]
+            for side in (1, -1):
+                sources.append(ring_slot(index, side, 0, 0, ep + off, whole)[0])
+            if off != 0:
+                line_merge(index, 0, off, sources, block(0, off, whole))
+            elif kind == "line":
+                line_merge(index, 0, 0, sources, out_ref.at[:, pl.ds(c0, cols)])
+            else:
+                add(out_ref.at[:, pl.ds(c0, cols)], sources)
+
+    def scatter_line(index, q, off):
+        _, c0, cols, _ = outof[index]
+        line_merge(index, q, off, [block(q, off, (c0, cols))], block(q, off, (c0, cols)))
+
+    note_own()
+    for what, index, q, off, d in gather_order(into, nplane, nep):
+        if what == "note line":
+            note_line(off)
+        elif what == "note ring":
+            note_ring(off, d)
+        elif what == "tables":
+            tables()
+        elif what == "own":
+            gather_own(index)
+        elif what == "line":
+            gather_line(index, q, off)
+        elif what == "ring":
+            gather_ring(index, off, d)
+        elif what == "pick":
+            pick(index)
+        else:
+            product(index, q)
+    activate()
+    weight_copies[2].wait()
+    for what, index, q, off, d in scatter_order(outof, nplane, nep):
+        if what == "down":
+            down(index)
+        elif what == "spread":
+            spread(index)
+        elif what == "ring":
+            scatter_ring(index, off, d)
+        else:
+            scatter_line(index, q, off)
+    count_copy().wait_recv()
+    load_ref[...] = (count_own[0] + count_in[...])[0:1, 0:2] / top
+    for cond, make in waits:
+        when(cond, lambda: make().wait_send())
+
+def copies_of(parts, nplane, nep):
+    far = nplane // 2
+    spots = 2 * nep - 1
+    notes = 2 + min(far, 2) + (spots - 1) * (1 + min(far, 2)) + spots * max(2 * far - 3, 0)
+    sent, returned = 0, 0
+    for kind, _, _, _ in parts:
+        ring = 2 + 2 * min(far - 1, 1) + sum(2 if d + 1 == far else 4 for d in range(1, far))
+        if kind == "line":
+            sent += 4 + 3 * (spots - 1) + 2 * spots * (far - 1)
+            returned += spots * ring + spots - 1
+        else:
+            sent += 4 + 6 * (far - 1) + 2 + nplane * (spots - 1)
+            returned += nplane * (spots - 1) + ring
+    return notes, sent, returned
+
+
+def layer(tokens, ids, picks, gates, hot, w_gate, w_up, w_down, plan, shapes):
+    nplane, nep, _, into, outof = plan
+    far = nplane // 2
+    count = nplane * nep
+    rows, width = tokens.shape
+    dma = pltpu.SemaphoreType.DMA
+    vmem = pl.BlockSpec(memory_space=pltpu.VMEM)
+    hbm = pl.BlockSpec(memory_space=pl.ANY)
+    notes, sent, _ = copies_of(into, nplane, nep)
+    returned = copies_of(outof, nplane, nep)[2]
+    swaps = len(into) + len(outof) + 1
+    return pl.pallas_call(
+        functools.partial(layer_kernel, plan),
+        out_shape=[
+            jax.ShapeDtypeStruct((rows, width), tokens.dtype),
+            jax.ShapeDtypeStruct((1, 2), jnp.float32),
+        ],
+        in_specs=[pl.BlockSpec(memory_space=pltpu.SMEM), hbm, vmem, vmem, vmem, hbm, hbm, hbm],
+        out_specs=[vmem, vmem],
+        scratch_shapes=[pltpu.VMEM(shape, kind) for shape, kind in shapes] + [
+            dma((len(into),)), dma((3,)), dma((count,)), dma((notes,)),
+            dma((len(into), 2, count)), dma((sent,)), dma((swaps,)), dma((swaps,)),
+            dma((len(outof), 2, far, 2, nep)), dma((len(outof), 2, count)), dma((returned,)),
+        ],
+        compiler_params=pltpu.CompilerParams(
+            collective_id=2, has_side_effects=True, vmem_limit_bytes=VMEM_LIMIT
+        ),
+    )(hot, tokens, ids, picks, gates, w_gate, w_up, w_down)
+
+
+def buffers(nplane, nep, rows, width, top, hidden, cap, kind):
+    count = nplane * nep
+    total = count * rows
+    f32 = jnp.float32
+    return [
+        ((count, rows, width), kind), ((count, top, 128), f32), ((3, top, total), f32),
+        ((2 * cap, total), kind), ((total, 2 * cap), kind),
+        ((width, hidden), kind), ((width, hidden), kind), ((hidden, width), kind),
+        ((2 * cap, width), kind), ((cap, width), kind),
+        ((2 * cap, hidden), f32), ((2 * cap, hidden), f32), ((2 * cap, hidden), kind),
+        ((2 * cap, width), kind), ((cap, width), kind), ((count, rows, width), kind),
+        ((2, nplane // 2, nep, rows, width), kind), ((2, count, rows, width), kind),
+        ((2, 8, 128), f32), ((8, 128), f32),
+    ]
+
+
+def cuts(width, shares):
+    unit = 256
+    units = width // unit
+    total = sum(share for _, share, _ in shares)
+    made, at, seen = [], 0, 0
+    for kind, share, start in shares:
+        seen += share
+        end = units * seen // total
+        made.append((kind, at * unit, (end - at) * unit, start))
+        at = end
+    return tuple(made)
+
+
 def body(
     tokens, expert_ids, gate_scores, replica_pick, replica_hot, gate_weight, up_weight, down_weight
 ):
@@ -364,6 +1020,16 @@
     cut = width // 256 * 128
     back_cut = width * 11 // 14 // 128 * 128
 
+    hidden = gate_weight.shape[2]
+    plan_shapes = buffers(nplane, nep, tok_dev, width, top_count, hidden, capacity, tokens.dtype)
+    need = sum(math.prod(shape) * jnp.dtype(kind).itemsize for shape, kind in plan_shapes)
+    if nplane % 2 == 0 and need < VMEM_LIMIT * 7 // 8:
+        plan = (nplane, nep, most, cuts(width, INTO), cuts(width, OUTOF))
+        return layer(
+            tokens, expert_ids.T, replica_pick.T, gate_scores.T, replica_hot,
+            gate_weight[0], up_weight[0], down_weight[0], plan, plan_shapes,
+        )
+
     coded = expert_ids * (ngroup + 1) + replica_pick
     note = jnp.concatenate([coded.astype(jnp.float32), gate_scores], axis=1).reshape(-1, 128)
     every, notes = gather_plane(tokens, note, nplane, nep, cut)

time: 135 us -> 96.7 us (0.72)
  matrix products: 25.8 us -> 0 us
  other arithmetic: 5.89 us -> 0 us
  local copies, waits for them, and re-layouts: 8.08 us -> 2.79 us
  waiting for transfers between devices: 2.79 us -> 0 us
  Pallas kernels: 91.3 us -> 93.1 us
    dot_general x4 -> x0, matrix products: 25.8 us -> none  [the longest x1 10.8 us: body(): jnp.dot(hidden, down_weight[0], preferred_element_type=jnp.float32)]
    ppermute x2 -> x0, waiting for transfers between devices: 2.79 us -> none  [the longest x1 2.79 us: body(): lax.ppermute(picked[capacity:], 'group', swap)]
    div x1 -> x0, other arithmetic: 1.84 us -> none  [body(): loads = jnp.stack([primary_load, replica_load])[None, :] / top_count]
    pallas_call x2 -> x1, Pallas kernels: 91.3 us -> 93.1 us  [layer(): pl.pallas_call(functools.partial(layer_kernel, plan), out_shape=[jax.Shap...]
    reduce_sum x3 -> x0, other arithmetic: 1.58 us -> none  [the longest x1 1.39 us: body(): primary_load = jnp.sum(((ids == me) & ~replicated).astype(jnp.float32))]
    slice x4 -> x0, local copies, waits for them, and re-layouts: 1.51 us -> none  [the longest x1 1.15 us: body(): pair_out[:capacity]]
    another operation x4 -> x0, local copies, waits for them, and re-layouts: 1.35 us -> none  [the longest x1 1.04 us: body(): mine = routing.reshape(nplane, 2, nep * tok_dev, 2 * top_count)]
    unnamed x14 -> x2, local copies, waits for them, and re-layouts: 3.67 us -> 2.79 us
  transfers between devices with their start and end apart: 2 -> 0, of which waited for: 1 -> 0; matrix products, arithmetic and copies ran while one was open for 3% -> 0% of each run, Pallas kernels for 0% -> 0%
where the time goes in v1:
time: 96.7 us; the launch traced here: 96.5 us
  Pallas kernels  93.1 us (96%)
  local copies, waits for them, and re-layouts  2.79 us (3%)
    pallas_call x1, Pallas kernels, layer(): pl.pallas_call(functools.partial(layer_kernel, plan), out_shape=[jax.Shap...  93.1 us
    unnamed x2, local copies, waits for them, and re-layouts  2.79 us

profile of v1, /device:TPU:0, one launch (start us, length us, event | category | flops | bytes accessed | tf_op | source)
XLA Modules:
  0.0 96.5 jit_solution(4701551049579729131)
XLA Ops:
  0.6 93.1 %shard_map.95 = (bf16[32,3584]{1,0:T(8,128)(2,1)}, f32[1,2]{1,0:T(1,128)}) custom-call(s32[4]{0:T(128)} %hot_ref.1, bf16[32,3584]{1,0:T(8,128)(2,1)} %tok_ref.1, s32[8,32]{1,0:T(8,128)} %bitcast.9, s32[8,32]{1,0:T(8,128)} %bitcast.10, f32[8,32]{1,0:T(8,128)} %bitcast.11, bf16[3584,1024]{1,0:T(8,128)(2,1)} %bitcast.6, bf16[3584,1024]{1,0:T(8,128)(2,1)} %bitcast.7, ...), custom_call_target="tpu_custom_call" | custom-call | tf_op jit(solution)/shard_map/pallas_call | solution.py:956
  93.7 1.6 %copy.12 = bf16[32,3584]{1,0:T(8,128)(2,1)} copy(bf16[32,3584]{1,0:T(8,128)(2,1)} %get-tuple-element.4) | data formatting | bytes 458752
  95.3 1.1 %copy.13 = f32[1,2]{1,0:T(1,128)} copy(f32[1,2]{1,0:T(1,128)} %get-tuple-element.5) | data formatting | bytes 16

commit v2 on v1

--- a/solution.py
+++ b/solution.py
@@ -12,10 +12,12 @@
 MESH = pl.DeviceIdType.MESH
 
 LINE_STEP, RING_STEP, DEEP_STEP, PRODUCT_STEP = 1.1, 3.1, 2.3, 2.6
-SPREAD_STEP, BACK_RING, BACK_LINE, BACK_DEEP = 2.0, 2.0, 2.0, 2.0
+SPREAD_STEP, BACK_RING, BACK_LINE, BACK_DEEP = 1.1, 2.0, 0.7, 3.0
+BACK_LAST = 2.8
 PIECES = 2
-INTO = (("line", 4, 5.0), ("line", 4, 0.0), ("line", 3, 0.0), ("ring", 3, 0.0))
-OUTOF = (("ring", 3, 0.0), ("line", 4, 1.0), ("line", 4, 4.0), ("line", 3, 8.0))
+POOL = 12
+INTO = (("line", 4, 0.0), ("line", 4, 0.0), ("line", 3, 5.0), ("ring", 3, 0.0))
+OUTOF = (("ring", 3, 1.1), ("line", 4, 1.5), ("line", 4, 6.4), ("line", 3, 4.4))
 VMEM_LIMIT = 67043328
 
 
@@ -370,13 +372,6 @@
 def gather_order(parts, nplane, nep):
     far = nplane // 2
     events = []
-    for off in offsets(nep):
-        at = LINE_STEP * abs(off)
-        if off:
-            events.append((at, 1, ("note line", 0, 0, off, 0)))
-        for d in range(1, far + 1):
-            events.append((at + RING_STEP * d, 1 + d, ("note ring", 0, 0, off, d)))
-    events.append((LINE_STEP * (nep - 1) + RING_STEP * far, 2 + far, ("tables", 0, 0, 0, 0)))
     for index, (kind, _, _, start) in enumerate(parts):
         events.append((start, 0, ("own", index, 0, 0, 0)))
         last = start
@@ -396,9 +391,11 @@
                     at = start + RING_STEP * min(q, nplane - q) + DEEP_STEP * abs(off)
                     last = max(last, at)
                     events.append((at, 2 + far, ("line", index, q, off, 0)))
-        events.append((last, 3 + far, ("pick", index, 0, 0, 0)))
+        if index == 0:
+            events.append((last, 3 + far, ("tables", index, 0, 0, 0)))
+        events.append((last, 4 + far, ("pick", index, 0, 0, 0)))
         for piece in range(PIECES):
-            events.append((last + PRODUCT_STEP * (piece + 1), 4 + far, ("product", index, piece, 0, 0)))
+            events.append((last + PRODUCT_STEP * (piece + 1), 5 + far, ("product", index, piece, 0, 0)))
     events.sort()
     return [event for _, _, event in events]
 
@@ -413,10 +410,10 @@
         if kind == "line":
             for off in offsets(nep):
                 for d in range(far, -1, -1):
-                    at = begin + BACK_RING * (far - d)
-                    if d == 0:
-                        at = at + BACK_LINE * (nep - 1 - abs(off))
+                    at = begin + BACK_RING * (far - d) + BACK_LINE * (nep - 1 - abs(off))
                     events.append((at, 2 + nep - abs(off), ("ring", index, 0, off, d)))
+            at = begin + BACK_RING * far + BACK_LINE * (nep - 1) + BACK_LAST
+            events.append((at, 3 + nep, ("last", index, 0, 0, 0)))
         else:
             for q in range(nplane):
                 for off in offsets(nep):
@@ -431,9 +428,9 @@
 
 def layer_kernel(
     plan, hot_ref, tok_ref, ids_ref, picks_ref, gates_ref, wg_hbm, wu_hbm, wd_hbm, out_ref, load_ref,
-    xs, notes, route, sel, back, wg, wu, wd, inputs, stage, acc_g, acc_u, hidden, pairs, stage2, parts_ref,
-    ring_land, line_land, count_own, count_in,
-    own_sem, w_sem, note_recv, note_send, x_recv, x_send, swap_send, swap_recv, ring_recv, line_recv, out_send,
+    xs, sel, back, wg, wu, wd, inputs, stage, acc_g, acc_u, hidden, pairs, stage2, parts_ref,
+    ring_land, line_land, deep_land, count_own, count_in,
+    own_sem, w_sem, pool_ring, pool_line, x_ring, x_line, swap_send, swap_recv, ring_recv, line_recv, deep_recv,
 ):
     nplane, nep, most, into, outof = plan
     far = nplane // 2
@@ -478,22 +475,38 @@
         else:
             pl.when(cond)(run)
 
-    waits = []
+    pools = {key: [] for key in (("ring", 1), ("ring", -1), ("line", 1), ("line", -1))}
+    swaps = []
 
     def copy(src, dst, send, recv, target):
         return pltpu.make_async_remote_copy(
             src_ref=src, dst_ref=dst, send_sem=send, recv_sem=recv, device_id=target, device_id_type=MESH
         )
 
-    def launch(cond, make):
-        when(cond, lambda: make().start())
-        waits.append((cond, make))
-
+    def send_out(cond, kind, side, make):
+        pool = pools[kind, side]
+        sems = (pool_ring if kind == "ring" else pool_line).at[0 if side > 0 else 1]
+        turn = len(pool) % sems.shape[0]
+        if len(pool) >= sems.shape[0]:
+            old_cond, old = pool[-sems.shape[0]]
+            when(old_cond, lambda: old().wait_send())
+
+        def ready():
+            return make(sems.at[turn])
+
+        when(cond, lambda: ready().start())
+        pool.append((cond, ready))
+
+    def swap(make):
+        make().start()
+        swaps.append(make)
+
+    lead = xs.shape[2] - width
     own_block = me_ring * nep + ep
     own_copies = []
     for index, (_, c0, cols, _) in enumerate(into):
         made = pltpu.make_async_copy(
-            tok_ref.at[:, pl.ds(c0, cols)], xs.at[own_block, :, pl.ds(c0, cols)], own_sem.at[index]
+            tok_ref.at[:, pl.ds(c0, cols)], xs.at[own_block, :, pl.ds(lead + c0, cols)], own_sem.at[index]
         )
         made.start()
         own_copies.append(made)
@@ -511,121 +524,77 @@
         def _(side=side):
             pl.semaphore_signal(barrier, inc=1, device_id=line_peers[side], device_id_type=MESH)
 
-    note = notes.at[own_block]
-    note[...] = jnp.zeros(note.shape, f32)
-    note[:, pl.ds(0, rows)] = ids_ref[...].astype(f32)
-    note[:, pl.ds(rows, rows)] = picks_ref[...].astype(f32)
-    note[:, pl.ds(2 * rows, rows)] = gates_ref[...]
+    own = jnp.concatenate(
+        [ids_ref[...].astype(f32), picks_ref[...].astype(f32), gates_ref[...]], axis=0
+    )
+    own = jnp.concatenate([own, jnp.zeros((3 * top, lead - rows), f32)], axis=1)
+    own = jnp.concatenate([own, jnp.zeros((lead - 3 * top, lead), f32)], axis=0)
+    xs[own_block, :, pl.ds(0, lead)] = own.T[:rows].astype(bf16)
     pl.semaphore_wait(barrier, 3 + has[1].astype(jnp.int32) + has[-1].astype(jnp.int32))
 
-    used = {"note": 0, "x": 0, "out": 0}
-
-    def place(index, half, block):
-        return x_recv.at[index, half, block]
-
-    def x_copy(index, half, block, cols, send, target):
+    def span_of(index):
+        _, c0, cols, _ = into[index]
+        return (0, lead + cols) if c0 == 0 else (lead + c0, cols)
+
+    def x_launch(cond, sem, kind, side, block, cols, target):
         part = xs.at[block, :, pl.ds(cols[0], cols[1])]
-        return copy(part, part, x_send.at[send], place(index, half, block), target)
-
-    def x_launch(cond, index, half, block, cols, target):
-        send = used["x"]
-        used["x"] += 1
-        launch(cond, lambda: x_copy(index, half, block, cols, send, target))
-
-    def x_wait(index, half, block, cols):
-        x_copy(index, half, block, cols, 0, partner).wait_recv()
+        send_out(cond, kind, side, lambda send: copy(part, part, send, sem, target))
+
+    def x_wait(sem, blocks, cols):
+        part = xs.at[pl.ds(0, blocks), :, pl.ds(cols[0], cols[1])]
+        copy(part, part, pool_ring.at[0, 0], sem, partner).wait_recv()
 
     def halves(c0, cols):
-        return {1: (0, (c0, cols // 2)), -1: (1, (c0 + cols // 2, cols // 2))}
-
-    def ring_out(cond, index, block, side, d):
-        _, c0, cols, _ = into[index]
-        half, span = (0, (c0, cols)) if d < far else halves(c0, cols)[side]
-        x_launch(cond, index, half, block, span, peers[side])
+        low = cols // 256 * 128
+        return {1: (c0, low), -1: (c0 + low, cols - low)}
+
+    starts_x = [0]
+    for kind, _, _, _ in into:
+        starts_x.append(starts_x[-1] + (nep if kind == "line" else count))
+
+    def line_sem(index, q, off):
+        at = starts_x[index] + ep + off
+        return x_line.at[at if into[index][0] == "line" else at + spot(q) * nep]
+
+    def ring_out(cond, index, block, off, side, d):
+        span = span_of(index) if d < far else halves(*span_of(index))[side]
+        x_launch(cond, x_ring.at[index, d - 1, ep + off], "ring", side, block, span, peers[side])
 
     def line_out(index, q, off, side):
-        _, c0, cols, _ = into[index]
         cond = both(valid(off), has[side])
-        x_launch(cond, index, 0, spot(q) * nep + ep + off, (c0, cols), line_peers[side])
-
-    def note_launch(cond, block, target):
-        send = used["note"]
-        used["note"] += 1
-        launch(cond, lambda: copy(
-            notes.at[block], notes.at[block], note_send.at[send], note_recv.at[block], target))
-
-    def note_wait(block):
-        copy(notes.at[block], notes.at[block], note_send.at[0], note_recv.at[block], partner).wait_recv()
-
-    def note_own():
-        for side in (1, -1):
-            note_launch(has[side], own_block, line_peers[side])
-        for side in (1, -1):
-            if far > 1 or side > 0:
-                note_launch(None, own_block, peers[side])
-
-    def note_line(off):
-        block = me_ring * nep + ep + off
-        when(valid(off), lambda: note_wait(block))
-        side = 1 if off < 0 else -1
-        note_launch(both(valid(off), has[side]), block, line_peers[side])
-        for way in (1, -1):
-            if far > 1 or way > 0:
-                note_launch(valid(off), block, peers[way])
-
-    def note_ring(off, d):
-        for side in (1, -1):
-            if d == far and side < 0:
-                continue
-            block = spot(-side * d) * nep + ep + off
-            when(valid(off), lambda: note_wait(block))
-            if d < far and (d + 1 < far or side > 0):
-                note_launch(valid(off), block, peers[side])
+        block = spot(q) * nep + ep + off
+        x_launch(cond, line_sem(index, q, off), "line", side, block, span_of(index), line_peers[side])
 
     def gather_own(index):
         own_copies[index].wait()
         for side in (1, -1):
             line_out(index, 0, 0, side)
         for side in (1, -1):
-            ring_out(None, index, own_block, side, 1)
+            ring_out(None, index, own_block, 0, side, 1)
 
     def gather_line(index, q, off):
-        kind, c0, cols, _ = into[index]
         block = spot(q) * nep + ep + off
-        when(valid(off), lambda: x_wait(index, 0, block, (c0, cols)))
+        when(valid(off), lambda: x_wait(line_sem(index, q, off), 1, span_of(index)))
         line_out(index, q, off, 1 if off < 0 else -1)
-        if kind == "line":
+        if into[index][0] == "line":
             for side in (1, -1):
-                ring_out(valid(off), index, block, side, 1)
+                ring_out(valid(off), index, block, off, side, 1)
 
     def gather_ring(index, off, d):
-        kind, c0, cols, _ = into[index]
+        sem = x_ring.at[index, d - 1, ep + off]
+        when(valid(off), lambda: x_wait(sem, 2 if d < far else 1, span_of(index)))
         for side in (1, -1):
-            block = spot(-side * d) * nep + ep + off
-            half, span = (0, (c0, cols)) if d < far else halves(c0, cols)[side]
-            when(valid(off), lambda: x_wait(index, half, block, span))
             if d < far:
-                ring_out(valid(off), index, block, side, d + 1)
-                if kind == "ring":
+                block = spot(-side * d) * nep + ep + off
+                ring_out(valid(off), index, block, off, side, d + 1)
+                if into[index][0] == "ring":
                     for way in (1, -1):
                         line_out(index, -side * d, 0, way)
-        if d == far and kind == "ring":
+        if d == far and into[index][0] == "ring":
             for way in (1, -1):
                 line_out(index, far, 0, way)
 
     def tables():
-        lane = lax.broadcasted_iota(jnp.int32, (top, 128), 1)
-        fit = 128 // rows
-        for chunk in range(total // 128):
-            for what in range(3):
-                piece = jnp.zeros((top, 128), f32)
-                for j in range(fit):
-                    tile = notes[chunk * fit + j]
-                    turn = (rows * (j - what)) % 128
-                    if turn:
-                        tile = pltpu.roll(tile, turn, 1)
-                    piece = jnp.where(lax.div(lane, rows) == j, tile, piece)
-                route[what, :, pl.ds(chunk * 128, 128)] = piece
         expert = group * nep + ep
         other = partner_group * nep + ep
         hot = (hot_ref[ep] * nep + ep).astype(f32)
@@ -644,7 +613,9 @@
 
         for chunk in range(total // 128):
             at = pl.ds(chunk * 128, 128)
-            ids, picks, gates = route[0, :, at], route[1, :, at], route[2, :, at]
+            fit = 128 // rows
+            tile = xs[pl.ds(chunk * fit, fit), :, pl.ds(0, lead)].reshape(128, lead).astype(f32).T
+            ids, picks, gates = tile[:top], tile[top:2 * top], tile[2 * top:3 * top]
             chosen = [ids == expert_f, ids == other_f]
             flag = [jnp.sum(c.astype(f32), axis=0, keepdims=True) for c in chosen]
             scale = [jnp.sum(jnp.where(c, gates, 0.0), axis=0, keepdims=True) for c in chosen]
@@ -665,7 +636,7 @@
         lane_n = lane8
         count_own[0] = jnp.where(lane_n == 0, sums[0], jnp.where(lane_n == 1, sums[1], 0.0))
         count_own[1] = jnp.where(lane_n == 0, sums[2], jnp.where(lane_n == 1, sums[3], 0.0))
-        launch(None, count_copy)
+        swap(count_copy)
 
     def count_copy():
         spare = len(into) + len(outof)
@@ -685,13 +656,14 @@
 
         def part(i, _):
             at = pl.ds(pl.multiple_of(c0 + i * step, step), step)
-            got = jnp.dot(sel[...], xs[:, :, at].reshape(total, step), preferred_element_type=f32).astype(bf16)
+            here = pl.ds(pl.multiple_of(lead + c0 + i * step, 128), step)
+            got = jnp.dot(sel[...], xs[:, :, here].reshape(total, step), preferred_element_type=f32).astype(bf16)
             inputs[pl.ds(0, cap), at] = got[:cap]
             stage[:, at] = got[cap:]
             return 0
 
         lax.fori_loop(0, cols // step, part, 0)
-        launch(None, lambda: in_copy(index))
+        swap(lambda: in_copy(index))
 
     seen = []
 
@@ -745,7 +717,7 @@
             return 0
 
         lax.fori_loop(0, cols // step, part, 0)
-        launch(None, lambda: back_copy(index))
+        swap(lambda: back_copy(index))
 
     def spread(index):
         _, c0, cols, _ = outof[index]
@@ -770,83 +742,96 @@
 
         lax.fori_loop(0, rows // 16, part, 0)
 
-    def out_launch(cond, src, dst, recv, target):
-        send = used["out"]
-        used["out"] += 1
-        launch(cond, lambda: copy(src, dst, out_send.at[send], recv, target))
-
     def way(side):
         return 0 if side > 0 else 1
 
-    def ring_slot(index, side, d, half, e, span):
-        c0, cols = span
-        return (
-            ring_land.at[way(side), d, e, :, pl.ds(c0, cols)],
-            ring_recv.at[index, way(side), d, half, e],
+    starts_r = [0]
+    for kind, _, _, _ in outof:
+        starts_r.append(starts_r[-1] + (nep if kind == "line" else 1))
+
+    def ring_sem(index, d, off):
+        return ring_recv.at[starts_r[index] + (ep + off if outof[index][0] == "line" else 0), d]
+
+    def ring_slot(side, d, off, span):
+        return ring_land.at[way(side), d, ep + off, :, pl.ds(span[0], span[1])]
+
+    def ring_send(cond, index, off, side, d, span):
+        dst = ring_slot(side, d - 1, off, span)
+        src = block(side * d, off, span)
+        send_out(
+            cond, "ring", side, lambda send: copy(src, dst, send, ring_sem(index, d - 1, off), peers[side])
         )
 
-    def ring_send(cond, index, off, side, d, half, span):
-        dst, recv = ring_slot(index, side, d - 1, half, ep + off, span)
-        src = parts_ref.at[spot(side * d) * nep + ep + off, :, pl.ds(span[0], span[1])]
-        out_launch(cond, src, dst, recv, peers[side])
-
-    def ring_await(index, off, side, d, half, span):
-        dst, recv = ring_slot(index, side, d, half, ep + off, span)
-        copy(dst, dst, out_send.at[0], recv, partner).wait_recv()
-        return dst
-
-    def line_slot(index, side, q, e, span):
-        c0, cols = span
-        return (
-            line_land.at[way(side), spot(q) * nep + e, :, pl.ds(c0, cols)],
-            line_recv.at[index, way(side), spot(q) * nep + e],
+    def ring_await(index, off, d, blocks):
+        _, c0, cols, _ = outof[index]
+        part = ring_land.at[0, 0, pl.ds(0, blocks), :, pl.ds(c0, cols)]
+        copy(part, part, pool_ring.at[0, 0], ring_sem(index, d, off), partner).wait_recv()
+
+    def deep_slot(side, q, off, span):
+        return deep_land.at[way(side), spot(q) * nep + ep + off, :, pl.ds(span[0], span[1])]
+
+    def deep_sem(index, side, q, off):
+        return deep_recv.at[deep_of[index], way(side), spot(q) * nep + ep + off]
+
+    deep_of, lined = {}, {}
+    for index, (kind, _, _, _) in enumerate(outof):
+        if kind == "line":
+            lined[index] = len(lined)
+        else:
+            deep_of[index] = len(deep_of)
+
+    def deep_send(cond, index, q, off, side):
+        _, c0, cols, _ = outof[index]
+        src, dst = block(q, off, (c0, cols)), deep_slot(side, q, off, (c0, cols))
+        send_out(
+            cond, "line", side, lambda send: copy(src, dst, send, deep_sem(index, side, q, off), line_peers[side])
         )
 
-    def line_send(cond, index, q, off, side):
+    def deep_await(index, side, q, off):
         _, c0, cols, _ = outof[index]
-        dst, recv = line_slot(index, side, q, ep + off, (c0, cols))
-        src = parts_ref.at[spot(q) * nep + ep + off, :, pl.ds(c0, cols)]
-        out_launch(cond, src, dst, recv, line_peers[side])
-
-    def line_await(index, side, q, off):
+        part = deep_slot(side, q, off, (c0, cols))
+        copy(part, part, pool_ring.at[0, 0], deep_sem(index, side, q, off), partner).wait_recv()
+        return part
+
+    def line_direct(index, off):
         _, c0, cols, _ = outof[index]
-        dst, recv = line_slot(index, side, q, ep + off, (c0, cols))
-        copy(dst, dst, out_send.at[0], recv, partner).wait_recv()
-        return dst
+        src, dst = block(0, off, (c0, cols)), line_land.at[ep, :, pl.ds(c0, cols)]
+        sem = line_recv.at[lined[index]]
+        side = 1 if off > 0 else -1
+        send_out(valid(off), "line", side, lambda send: copy(src, dst, send, sem, (group, ep + off)))
 
     def block(q, off, span):
         return parts_ref.at[spot(q) * nep + ep + off, :, pl.ds(span[0], span[1])]
 
-    def line_merge(index, q, off, sources, dst):
-        left, right = has[-1], has[1]
+    def scatter_line(index, q, off):
+        _, c0, cols, _ = outof[index]
+        here = block(q, off, (c0, cols))
         if off != 0:
             side = 1 if off > 0 else -1
             behind = has[-side]
 
-            def go():
-                @pl.when(behind)
-                def _():
-                    add(dst, sources + [line_await(index, side, q, off)])
-
-                if len(sources) > 1:
-                    @pl.when(jnp.logical_not(behind))
-                    def _():
-                        add(dst, sources)
-
-            when(valid(off), go)
-            line_send(valid(off), index, q, off, side)
+            @pl.when(both(valid(off), behind))
+            def _():
+                add(here, [here, deep_await(index, side, q, off)])
+
+            deep_send(valid(off), index, q, off, side)
         else:
+            left, right = has[-1], has[1]
+
             @pl.when(left & right)
             def _():
-                add(dst, sources + [line_await(index, 1, q, 0), line_await(index, -1, q, 0)])
+                add(here, [here, deep_await(index, 1, q, 0), deep_await(index, -1, q, 0)])
 
             @pl.when(left & jnp.logical_not(right))
             def _():
-                add(dst, sources + [line_await(index, 1, q, 0)])
+                add(here, [here, deep_await(index, 1, q, 0)])
 
             @pl.when(right & jnp.logical_not(left))
             def _():
-                add(dst, sources + [line_await(index, -1, q, 0)])
+                add(here, [here, deep_await(index, -1, q, 0)])
+
+    def plane_terms(off, span):
+        return [block(0, off, span)] + [ring_slot(side, 0, off, span) for side in (1, -1)]
 
     def scatter_ring(index, off, d):
         kind, c0, cols, _ = outof[index]
@@ -854,51 +839,38 @@
         split = halves(c0, cols)
         if d == far:
             for side in (1, -1):
-                half, span = split[side]
-                ring_send(valid(off), index, off, side, d, half, span)
+                ring_send(valid(off), index, off, side, d, split[side])
             if far > 1:
                 for side in (1, -1):
-                    half, span = split[-side]
-                    ring_send(valid(off), index, off, side, d - 1, half, span)
+                    ring_send(valid(off), index, off, side, d - 1, split[-side])
         elif d > 0:
+            when(valid(off), lambda: ring_await(index, off, d, 1 if d + 1 == far else 2))
             for side in (1, -1):
-                pieces = [split[side]] if d + 1 == far else [split[1], split[-1]]
-                for half, span in pieces:
-                    def go(half=half, span=span, side=side):
-                        got = ring_await(index, off, side, d, half, span)
-                        add(block(side * d, off, span), [block(side * d, off, span), got])
+                for span in [split[side]] if d + 1 == far else [whole]:
+                    def go(side=side, span=span):
+                        here = block(side * d, off, span)
+                        add(here, [here, ring_slot(side, d, off, span)])
 
                     when(valid(off), go)
-                    ring_send(valid(off), index, off, side, d, half, span)
+                    ring_send(valid(off), index, off, side, d, span)
         else:
-            def take():
-                pieces = {}
-                for side in (1, -1):
-                    for half, span in ([split[side]] if far == 1 else [split[1], split[-1]]):
-                        ring_await(index, off, side, 0, half, span)
-
-            when(valid(off), take)
-            sources = [block(0, off, whole)]
-            for side in (1, -1):
-                sources.append(ring_slot(index, side, 0, 0, ep + off, whole)[0])
+            when(valid(off), lambda: ring_await(index, off, 0, 1 if far == 1 else 2))
             if off != 0:
-                line_merge(index, 0, off, sources, block(0, off, whole))
-            elif kind == "line":
-                line_merge(index, 0, 0, sources, out_ref.at[:, pl.ds(c0, cols)])
-            else:
-                add(out_ref.at[:, pl.ds(c0, cols)], sources)
-
-    def scatter_line(index, q, off):
+                when(valid(off), lambda: add(block(0, off, whole), plane_terms(off, whole)))
+                line_direct(index, off)
+            elif kind == "ring":
+                add(out_ref.at[:, pl.ds(c0, cols)], plane_terms(0, whole))
+
+    def scatter_last(index):
         _, c0, cols, _ = outof[index]
-        line_merge(index, q, off, [block(q, off, (c0, cols))], block(q, off, (c0, cols)))
-
-    note_own()
+        at = pl.ds(c0, cols)
+        part = line_land.at[pl.ds(0, nep - 1), :, at]
+        copy(part, part, pool_line.at[0, 0], line_recv.at[lined[index]], partner).wait_recv()
+        others = [line_land.at[lax.rem(ep + step, nep), :, at] for step in range(1, nep)]
+        add(out_ref.at[:, at], plane_terms(0, (c0, cols)) + others)
+
     for what, index, q, off, d in gather_order(into, nplane, nep):
-        if what == "note line":
-            note_line(off)
-        elif what == "note ring":
-            note_ring(off, d)
-        elif what == "tables":
+        if what == "tables":
             tables()
         elif what == "own":
             gather_own(index)
@@ -919,28 +891,17 @@
             spread(index)
         elif what == "ring":
             scatter_ring(index, off, d)
+        elif what == "last":
+            scatter_last(index)
         else:
             scatter_line(index, q, off)
     count_copy().wait_recv()
     load_ref[...] = (count_own[0] + count_in[...])[0:1, 0:2] / top
-    for cond, make in waits:
-        when(cond, lambda: make().wait_send())
-
-def copies_of(parts, nplane, nep):
-    far = nplane // 2
-    spots = 2 * nep - 1
-    notes = 2 + min(far, 2) + (spots - 1) * (1 + min(far, 2)) + spots * max(2 * far - 3, 0)
-    sent, returned = 0, 0
-    for kind, _, _, _ in parts:
-        ring = 2 + 2 * min(far - 1, 1) + sum(2 if d + 1 == far else 4 for d in range(1, far))
-        if kind == "line":
-            sent += 4 + 3 * (spots - 1) + 2 * spots * (far - 1)
-            returned += spots * ring + spots - 1
-        else:
-            sent += 4 + 6 * (far - 1) + 2 + nplane * (spots - 1)
-            returned += nplane * (spots - 1) + ring
-    return notes, sent, returned
-
+    for make in swaps:
+        make().wait_send()
+    for (kind, _), pool in pools.items():
+        for cond, make in pool[-(pool_ring if kind == "ring" else pool_line).shape[1]:]:
+            when(cond, lambda: make().wait_send())
 
 def layer(tokens, ids, picks, gates, hot, w_gate, w_up, w_down, plan, shapes):
     nplane, nep, _, into, outof = plan
@@ -950,8 +911,9 @@
     dma = pltpu.SemaphoreType.DMA
     vmem = pl.BlockSpec(memory_space=pltpu.VMEM)
     hbm = pl.BlockSpec(memory_space=pl.ANY)
-    notes, sent, _ = copies_of(into, nplane, nep)
-    returned = copies_of(outof, nplane, nep)[2]
+    lines_in = sum(kind == "line" for kind, _, _, _ in into)
+    lines_out = sum(kind == "line" for kind, _, _, _ in outof)
+    rings_in, rings_out = len(into) - lines_in, len(outof) - lines_out
     swaps = len(into) + len(outof) + 1
     return pl.pallas_call(
         functools.partial(layer_kernel, plan),
@@ -962,9 +924,9 @@
         in_specs=[pl.BlockSpec(memory_space=pltpu.SMEM), hbm, vmem, vmem, vmem, hbm, hbm, hbm],
         out_specs=[vmem, vmem],
         scratch_shapes=[pltpu.VMEM(shape, kind) for shape, kind in shapes] + [
-            dma((len(into),)), dma((3,)), dma((count,)), dma((notes,)),
-            dma((len(into), 2, count)), dma((sent,)), dma((swaps,)), dma((swaps,)),
-            dma((len(outof), 2, far, 2, nep)), dma((len(outof), 2, count)), dma((returned,)),
+            dma((len(into),)), dma((3,)), dma((2, POOL)), dma((2, POOL)),
+            dma((len(into), far, nep)), dma((lines_in * nep + rings_in * count,)), dma((swaps,)), dma((swaps,)),
+            dma((lines_out * nep + rings_out, far)), dma((lines_out,)), dma((rings_out, 2, count)),
         ],
         compiler_params=pltpu.CompilerParams(
             collective_id=2, has_side_effects=True, vmem_limit_bytes=VMEM_LIMIT
@@ -977,13 +939,14 @@
     total = count * rows
     f32 = jnp.float32
     return [
-        ((count, rows, width), kind), ((count, top, 128), f32), ((3, top, total), f32),
+        ((count, rows, width + 128), kind),
         ((2 * cap, total), kind), ((total, 2 * cap), kind),
         ((width, hidden), kind), ((width, hidden), kind), ((hidden, width), kind),
         ((2 * cap, width), kind), ((cap, width), kind),
         ((2 * cap, hidden), f32), ((2 * cap, hidden), f32), ((2 * cap, hidden), kind),
         ((2 * cap, width), kind), ((cap, width), kind), ((count, rows, width), kind),
-        ((2, nplane // 2, nep, rows, width), kind), ((2, count, rows, width), kind),
+        ((2, nplane // 2, nep, rows, width), kind), ((nep, rows, width), kind),
+        ((2, count, rows, width), kind),
         ((2, 8, 128), f32), ((8, 128), f32),
     ]
 
@@ -1023,7 +986,7 @@
     hidden = gate_weight.shape[2]
     plan_shapes = buffers(nplane, nep, tok_dev, width, top_count, hidden, capacity, tokens.dtype)
     need = sum(math.prod(shape) * jnp.dtype(kind).itemsize for shape, kind in plan_shapes)
-    if nplane % 2 == 0 and need < VMEM_LIMIT * 7 // 8:
+    if nplane % 2 == 0 and nplane > 2 and device_count <= 256 and need < VMEM_LIMIT * 7 // 8:
         plan = (nplane, nep, most, cuts(width, INTO), cuts(width, OUTOF))
         return layer(
             tokens, expert_ids.T, replica_pick.T, gate_scores.T, replica_hot,

time: 96.7 us -> 85.4 us (0.88)
  Pallas kernels: 93.1 us -> 81.8 us
    pallas_call x1, Pallas kernels: 93.1 us -> 81.8 us  [layer(): pl.pallas_call(functools.partial(layer_kernel, plan), out_shape=[jax.Shap...]
where the time goes in v2:
time: 85.4 us; the launch traced here: 85.2 us
  Pallas kernels  81.8 us (96%)
  local copies, waits for them, and re-layouts  2.79 us (3%)
    pallas_call x1, Pallas kernels, layer(): pl.pallas_call(functools.partial(layer_kernel, plan), out_shape=[jax.Shap...  81.8 us
    unnamed x2, local copies, waits for them, and re-layouts  2.79 us

profile of v2, /device:TPU:0, one launch (start us, length us, event | category | flops | bytes accessed | tf_op | source)
XLA Modules:
  0.0 85.2 jit_solution(8418759237244479538)
XLA Ops:
  0.6 81.8 %shard_map.95 = (bf16[32,3584]{1,0:T(8,128)(2,1)}, f32[1,2]{1,0:T(1,128)}) custom-call(s32[4]{0:T(128)} %hot_ref.1, bf16[32,3584]{1,0:T(8,128)(2,1)} %tok_ref.1, s32[8,32]{1,0:T(8,128)} %bitcast.9, s32[8,32]{1,0:T(8,128)} %bitcast.10, f32[8,32]{1,0:T(8,128)} %bitcast.11, bf16[3584,1024]{1,0:T(8,128)(2,1)} %bitcast.6, bf16[3584,1024]{1,0:T(8,128)(2,1)} %bitcast.7, ...), custom_call_target="tpu_custom_call" | custom-call | tf_op jit(solution)/shard_map/pallas_call | solution.py:918
  82.4 1.6 %copy.12 = bf16[32,3584]{1,0:T(8,128)(2,1)} copy(bf16[32,3584]{1,0:T(8,128)(2,1)} %get-tuple-element.4) | data formatting | bytes 458752
  84.1 1.1 %copy.13 = f32[1,2]{1,0:T(1,128)} copy(f32[1,2]{1,0:T(1,128)} %get-tuple-element.5) | data formatting | bytes 16

commit v3 on v2

--- a/solution.py
+++ b/solution.py
@@ -11,14 +11,15 @@
 AXES = ("group", "ep")
 MESH = pl.DeviceIdType.MESH
 
-LINE_STEP, RING_STEP, DEEP_STEP, PRODUCT_STEP = 1.1, 3.1, 2.3, 2.6
+LINE_STEP, RING_STEP, DEEP_STEP, PRODUCT_STEP = 2.3, 6.0, 4.3, 3.1
 SPREAD_STEP, BACK_RING, BACK_LINE, BACK_DEEP = 1.1, 2.0, 0.7, 3.0
 BACK_LAST = 2.8
-PIECES = 2
+PIECES = 4
 POOL = 12
-INTO = (("line", 4, 0.0), ("line", 4, 0.0), ("line", 3, 5.0), ("ring", 3, 0.0))
+INTO = (("line", 3, 1.5), ("line", 3, 1.3), ("line", 3, 10.3), ("line", 2, 11.6), ("ring", 3, 1.6))
 OUTOF = (("ring", 3, 1.1), ("line", 4, 1.5), ("line", 4, 6.4), ("line", 3, 4.4))
 VMEM_LIMIT = 67043328
+SPARE = 3 * 2 ** 20
 
 
 def place_of(nplane, nep):
@@ -371,7 +372,7 @@
 
 def gather_order(parts, nplane, nep):
     far = nplane // 2
-    events = []
+    events, ready = [], 0.0
     for index, (kind, _, _, start) in enumerate(parts):
         events.append((start, 0, ("own", index, 0, 0, 0)))
         last = start
@@ -391,11 +392,12 @@
                     at = start + RING_STEP * min(q, nplane - q) + DEEP_STEP * abs(off)
                     last = max(last, at)
                     events.append((at, 2 + far, ("line", index, q, off, 0)))
+        ready = last if index == 0 else max(last, ready)
         if index == 0:
             events.append((last, 3 + far, ("tables", index, 0, 0, 0)))
-        events.append((last, 4 + far, ("pick", index, 0, 0, 0)))
+        events.append((ready, 4 + far, ("pick", index, 0, 0, 0)))
         for piece in range(PIECES):
-            events.append((last + PRODUCT_STEP * (piece + 1), 5 + far, ("product", index, piece, 0, 0)))
+            events.append((ready + PRODUCT_STEP * (piece + 1), 5 + far, ("product", index, piece, 0, 0)))
     events.sort()
     return [event for _, _, event in events]
 
@@ -427,10 +429,10 @@
 
 
 def layer_kernel(
-    plan, hot_ref, tok_ref, ids_ref, picks_ref, gates_ref, wg_hbm, wu_hbm, wd_hbm, out_ref, load_ref,
-    xs, sel, back, wg, wu, wd, inputs, stage, acc_g, acc_u, hidden, pairs, stage2, parts_ref,
+    plan, hot_hbm, tok_ref, ids_hbm, picks_hbm, gates_hbm, wg_hbm, wu_hbm, wd_hbm, out_ref, load_ref,
+    hot_ref, ids_ref, picks_ref, gates_ref, xs, sel, back, wg, wu, wd, inputs, stage, acc_g, acc_u, hidden, pairs, stage2, parts_ref,
     ring_land, line_land, deep_land, count_own, count_in,
-    own_sem, w_sem, pool_ring, pool_line, x_ring, x_line, swap_send, swap_recv, ring_recv, line_recv, deep_recv,
+    own_sem, small_sem, w_sem, pool_ring, pool_line, x_ring, x_line, swap_send, swap_recv, ring_recv, line_recv, deep_recv,
 ):
     nplane, nep, most, into, outof = plan
     far = nplane // 2
@@ -503,6 +505,13 @@
 
     lead = xs.shape[2] - width
     own_block = me_ring * nep + ep
+    small_copies = []
+    for index, (src, dst) in enumerate(
+        ((ids_hbm, ids_ref), (picks_hbm, picks_ref), (gates_hbm, gates_ref), (hot_hbm, hot_ref))
+    ):
+        made = pltpu.make_async_copy(src, dst, small_sem.at[index])
+        made.start()
+        small_copies.append(made)
     own_copies = []
     for index, (_, c0, cols, _) in enumerate(into):
         made = pltpu.make_async_copy(
@@ -524,6 +533,8 @@
         def _(side=side):
             pl.semaphore_signal(barrier, inc=1, device_id=line_peers[side], device_id_type=MESH)
 
+    for made in small_copies:
+        made.wait()
     own = jnp.concatenate(
         [ids_ref[...].astype(f32), picks_ref[...].astype(f32), gates_ref[...]], axis=0
     )
@@ -676,27 +687,24 @@
                 weight_copies[1].wait()
         first = piece not in seen
         seen.append(piece)
+        last = seen.count(piece) == len(into)
         tiles = acc_g.shape[1] // step // PIECES
 
         def part(j, _):
             at = pl.ds(pl.multiple_of((piece * tiles + j) * step, step), step)
+            acts = []
             for weight, acc in ((wg, acc_g), (wu, acc_u)):
                 got = jnp.dot(
                     inputs[:, pl.ds(c0, cols)], weight[pl.ds(c0, cols), at], preferred_element_type=f32
                 )
-                acc[:, at] = got if first else acc[:, at] + got
+                acts.append(got if first else acc[:, at] + got)
+            if last:
+                hidden[:, at] = (acts[0] / (1.0 + jnp.exp(-acts[0])) * acts[1]).astype(bf16)
+            else:
+                acc_g[:, at], acc_u[:, at] = acts
             return 0
 
         lax.fori_loop(0, tiles, part, 0)
-
-    def activate():
-        def part(i, _):
-            at = pl.ds(pl.multiple_of(i * 32, 32), 32)
-            gate = acc_g[at, :]
-            hidden[at, :] = (gate / (1.0 + jnp.exp(-gate)) * acc_u[at, :]).astype(bf16)
-            return 0
-
-        lax.fori_loop(0, 2 * cap // 32, part, 0)
 
     def back_copy(index):
         _, c0, cols, _ = outof[index]
@@ -882,7 +890,6 @@
             pick(index)
         else:
             product(index, q)
-    activate()
     weight_copies[2].wait()
     for what, index, q, off, d in scatter_order(outof, nplane, nep):
         if what == "down":
@@ -903,28 +910,41 @@
         for cond, make in pool[-(pool_ring if kind == "ring" else pool_line).shape[1]:]:
             when(cond, lambda: make().wait_send())
 
-def layer(tokens, ids, picks, gates, hot, w_gate, w_up, w_down, plan, shapes):
+def finish_kernel(mixed_in, load_in, mixed_out, load_out, mixed_here, load_here, sems):
+    trips = ((mixed_in, mixed_here, mixed_out), (load_in, load_here, load_out))
+    for way in range(2):
+        made = []
+        for index, trip in enumerate(trips):
+            made.append(pltpu.make_async_copy(trip[way], trip[way + 1], sems.at[way, index]))
+            made[-1].start()
+        for one in made:
+            one.wait()
+
+
+def layer(tokens, ids, picks, gates, hot, w_gate, w_up, w_down, plan, shapes, need):
     nplane, nep, _, into, outof = plan
     far = nplane // 2
     count = nplane * nep
     rows, width = tokens.shape
     dma = pltpu.SemaphoreType.DMA
     vmem = pl.BlockSpec(memory_space=pltpu.VMEM)
-    hbm = pl.BlockSpec(memory_space=pl.ANY)
+    hbm = pl.BlockSpec(memory_space=pltpu.HBM)
     lines_in = sum(kind == "line" for kind, _, _, _ in into)
     lines_out = sum(kind == "line" for kind, _, _, _ in outof)
     rings_in, rings_out = len(into) - lines_in, len(outof) - lines_out
     swaps = len(into) + len(outof) + 1
-    return pl.pallas_call(
+    mixed, loads = pl.pallas_call(
         functools.partial(layer_kernel, plan),
         out_shape=[
             jax.ShapeDtypeStruct((rows, width), tokens.dtype),
             jax.ShapeDtypeStruct((1, 2), jnp.float32),
         ],
-        in_specs=[pl.BlockSpec(memory_space=pltpu.SMEM), hbm, vmem, vmem, vmem, hbm, hbm, hbm],
+        in_specs=[hbm] * 8,
         out_specs=[vmem, vmem],
-        scratch_shapes=[pltpu.VMEM(shape, kind) for shape, kind in shapes] + [
-            dma((len(into),)), dma((3,)), dma((2, POOL)), dma((2, POOL)),
+        scratch_shapes=[pltpu.SMEM(hot.shape, hot.dtype)] + [
+            pltpu.VMEM(x.shape, x.dtype) for x in (ids, picks, gates)
+        ] + [pltpu.VMEM(shape, kind) for shape, kind in shapes] + [
+            dma((len(into),)), dma((4,)), dma((3,)), dma((2, POOL)), dma((2, POOL)),
             dma((len(into), far, nep)), dma((lines_in * nep + rings_in * count,)), dma((swaps,)), dma((swaps,)),
             dma((lines_out * nep + rings_out, far)), dma((lines_out,)), dma((rings_out, 2, count)),
         ],
@@ -932,6 +952,14 @@
             collective_id=2, has_side_effects=True, vmem_limit_bytes=VMEM_LIMIT
         ),
     )(hot, tokens, ids, picks, gates, w_gate, w_up, w_down)
+    return pl.pallas_call(
+        finish_kernel,
+        out_shape=[jax.ShapeDtypeStruct(x.shape, x.dtype) for x in (mixed, loads)],
+        in_specs=[hbm, hbm],
+        out_specs=[hbm, hbm],
+        scratch_shapes=[pltpu.VMEM(x.shape, x.dtype) for x in (mixed, loads)] + [dma((2, 2))],
+        compiler_params=pltpu.CompilerParams(vmem_limit_bytes=VMEM_LIMIT),
+    )(mixed, loads)
 
 
 def buffers(nplane, nep, rows, width, top, hidden, cap, kind):
@@ -990,7 +1018,7 @@
         plan = (nplane, nep, most, cuts(width, INTO), cuts(width, OUTOF))
         return layer(
             tokens, expert_ids.T, replica_pick.T, gate_scores.T, replica_hot,
-            gate_weight[0], up_weight[0], down_weight[0], plan, plan_shapes,
+            gate_weight[0], up_weight[0], down_weight[0], plan, plan_shapes, need,
         )
 
     coded = expert_ids * (ngroup + 1) + replica_pick

time: 85.4 us -> 81.5 us (0.954)
  local copies, waits for them, and re-layouts: 2.79 us -> 0 us
  Pallas kernels: 81.8 us -> 80.7 us
    unnamed x2 -> x0, local copies, waits for them, and re-layouts: 2.79 us -> none
    pallas_call x1, Pallas kernels: 81.8 us -> 79 us  [layer(): pl.pallas_call(functools.partial(layer_kernel, plan), out_shape=[jax.Shap...]
    pallas_call x0 -> x1, Pallas kernels: none -> 1.66 us  [layer(): pl.pallas_call(finish_kernel, out_shape=[jax.ShapeDtypeStruct(x.shape, x....]
where the time goes in v3:
time: 81.5 us; the launch traced here: 81.3 us
  Pallas kernels  80.7 us (99%)
    pallas_call x1, Pallas kernels, layer(): pl.pallas_call(functools.partial(layer_kernel, plan), out_shape=[jax.Shap...  79 us
    pallas_call x1, Pallas kernels, layer(): pl.pallas_call(finish_kernel, out_shape=[jax.ShapeDtypeStruct(x.shape, x....  1.66 us

profile of v3, /device:TPU:0, one launch (start us, length us, event | category | flops | bytes accessed | tf_op | source)
XLA Modules:
  0.0 81.3 jit_solution(963324120730543869)
XLA Ops:
  0.6 79.0 %shard_map.95 = (bf16[32,3584]{1,0:T(8,128)(2,1)}, f32[1,2]{1,0:T(1,128)}) custom-call(s32[4]{0:T(128)} %hot_hbm.1, bf16[32,3584]{1,0:T(8,128)(2,1)} %tok_ref.1, s32[8,32]{1,0:T(8,128)} %bitcast.9, s32[8,32]{1,0:T(8,128)} %bitcast.10, f32[8,32]{1,0:T(8,128)} %bitcast.11, bf16[3584,1024]{1,0:T(8,128)(2,1)} %bitcast.6, bf16[3584,1024]{1,0:T(8,128)(2,1)} %bitcast.7, ...), custom_call_target="tpu_custom_call" | custom-call | tf_op jit(solution)/shard_map/pallas_call | solution.py:936
  79.7 1.7 %shard_map.96 = (bf16[32,3584]{1,0:T(8,128)(2,1)}, f32[1,2]{1,0:T(1,128)}) custom-call(bf16[32,3584]{1,0:T(8,128)(2,1)} %get-tuple-element.4.mixed_in, f32[1,2]{1,0:T(1,128)} %get-tuple-element.5.load_in), custom_call_target="tpu_custom_call" | custom-call | tf_op jit(solution)/shard_map/pallas_call | solution.py:955

commit v4 on v3

--- a/solution.py
+++ b/solution.py
@@ -15,6 +15,7 @@
 SPREAD_STEP, BACK_RING, BACK_LINE, BACK_DEEP = 1.1, 2.0, 0.7, 3.0
 BACK_LAST = 2.8
 PIECES = 4
+STRIP, PICK_STEP = 256, 0.8
 POOL = 12
 INTO = (("line", 3, 1.5), ("line", 3, 1.3), ("line", 3, 10.3), ("line", 2, 11.6), ("ring", 3, 1.6))
 OUTOF = (("ring", 3, 1.1), ("line", 4, 1.5), ("line", 4, 6.4), ("line", 3, 4.4))
@@ -395,7 +396,8 @@
         ready = last if index == 0 else max(last, ready)
         if index == 0:
             events.append((last, 3 + far, ("tables", index, 0, 0, 0)))
-        events.append((ready, 4 + far, ("pick", index, 0, 0, 0)))
+        for strip in range(parts[index][2] // STRIP):
+            events.append((ready + PICK_STEP * strip, 4 + far, ("pick", index, strip, 0, 0)))
         for piece in range(PIECES):
             events.append((ready + PRODUCT_STEP * (piece + 1), 5 + far, ("product", index, piece, 0, 0)))
     events.sort()
@@ -662,19 +664,15 @@
             swap_send.at[index], swap_recv.at[index], partner,
         )
 
-    def pick(index):
+    def pick(index, strip):
         _, c0, cols, _ = into[index]
 
-        def part(i, _):
-            at = pl.ds(pl.multiple_of(c0 + i * step, step), step)
-            here = pl.ds(pl.multiple_of(lead + c0 + i * step, 128), step)
-            got = jnp.dot(sel[...], xs[:, :, here].reshape(total, step), preferred_element_type=f32).astype(bf16)
-            inputs[pl.ds(0, cap), at] = got[:cap]
-            stage[:, at] = got[cap:]
-            return 0
-
-        lax.fori_loop(0, cols // step, part, 0)
-        swap(lambda: in_copy(index))
+        at, here = pl.ds(c0 + strip * STRIP, STRIP), pl.ds(lead + c0 + strip * STRIP, STRIP)
+        got = jnp.dot(sel[...], xs[:, :, here].reshape(total, STRIP), preferred_element_type=f32).astype(bf16)
+        inputs[pl.ds(0, cap), at] = got[:cap]
+        stage[:, at] = got[cap:]
+        if strip == cols // STRIP - 1:
+            swap(lambda: in_copy(index))
 
     seen = []
 
@@ -887,7 +885,7 @@
         elif what == "ring":
             gather_ring(index, off, d)
         elif what == "pick":
-            pick(index)
+            pick(index, q)
         else:
             product(index, q)
     weight_copies[2].wait()

time: 81.5 us -> 81.1 us (level)
  no operation moved by 1% of the time
where the time goes in v4:
time: 81.1 us; the launch traced here: 80.9 us
  Pallas kernels  80.2 us (99%)
    pallas_call x1, Pallas kernels, layer(): pl.pallas_call(functools.partial(layer_kernel, plan), out_shape=[jax.Shap...  78.6 us
    pallas_call x1, Pallas kernels, layer(): pl.pallas_call(finish_kernel, out_shape=[jax.ShapeDtypeStruct(x.shape, x....  1.66 us

profile of v4, /device:TPU:0, one launch (start us, length us, event | category | flops | bytes accessed | tf_op | source)
XLA Modules:
  0.0 80.9 jit_solution(2503055551102911707)
XLA Ops:
  0.6 78.6 %shard_map.95 = (bf16[32,3584]{1,0:T(8,128)(2,1)}, f32[1,2]{1,0:T(1,128)}) custom-call(s32[4]{0:T(128)} %hot_hbm.1, bf16[32,3584]{1,0:T(8,128)(2,1)} %tok_ref.1, s32[8,32]{1,0:T(8,128)} %bitcast.9, s32[8,32]{1,0:T(8,128)} %bitcast.10, f32[8,32]{1,0:T(8,128)} %bitcast.11, bf16[3584,1024]{1,0:T(8,128)(2,1)} %bitcast.6, bf16[3584,1024]{1,0:T(8,128)(2,1)} %bitcast.7, ...), custom_call_target="tpu_custom_call" | custom-call | tf_op jit(solution)/shard_map/pallas_call | solution.py:934
  79.2 1.7 %shard_map.96 = (bf16[32,3584]{1,0:T(8,128)(2,1)}, f32[1,2]{1,0:T(1,128)}) custom-call(bf16[32,3584]{1,0:T(8,128)(2,1)} %get-tuple-element.4.mixed_in, f32[1,2]{1,0:T(1,128)} %get-tuple-element.5.load_in), custom_call_target="tpu_custom_call" | custom-call | tf_op jit(solution)/shard_map/pallas_call | solution.py:953
